TPU v7x, 32 devices: a whole 2x2x4 slice. The times are simulated.
32 devices in a mesh: ha: 4 (over y, x), wa: 8 (over z, core).
Axes of the slice: x: 2, y: 2, z: 4, core: 2. Of those that a mesh axis runs over, the one named last changes fastest.
Arguments:
- tokens: bfloat16 [112, 224, 384], P('ha', 'wa'), may hold values from -8 to 8
- cotangent: bfloat16 [112, 224, 384], P('ha', 'wa'), may hold values from -8 to 8
- w_qkv: bfloat16 [384, 1152], replicated, may hold values from -0.3125 to 0.3125
- w_proj: bfloat16 [384, 384], replicated, may hold values from -0.3125 to 0.3125
- w_fc1: bfloat16 [384, 1536], replicated, may hold values from -0.3125 to 0.3125
- w_fc2: bfloat16 [1536, 384], replicated, may hold values from -0.15625 to 0.15625
- bias_table: float32 [169, 12], replicated, may hold values from -4 to 280
- rel_index: int32 [49, 49], replicated, may hold values from 0 to 168, as said below
- region: int32 [112, 224], P('ha', 'wa'), may hold values from 0 to 15, as said below
Outputs:
- block_out: bfloat16 [112, 224, 384], P('ha', 'wa')
- token_grad: bfloat16 [112, 224, 384], P('ha', 'wa')
- grad_qkv: float32 [384, 1152], replicated
- grad_proj: float32 [384, 384], replicated
- grad_fc1: float32 [384, 1536], replicated
- grad_fc2: float32 [1536, 384], replicated
- grad_table: float32 [169, 12], replicated
Inputs may be any that keep to these rules, and one draw needn't show every extreme that they name: `rel_index`: pairs of window positions with the same offset share an entry, pairs with different offsets have different entries. `region`: the crop id of the token at each position of the shifted grid.
All inputs are finite; a program needn't handle non-finite values.
Results may differ from a plain program's by a relative error of at most 0.016.
Values may be sent and summed in bfloat16 or wider, within the bound.
A program may use at most 128 MiB of HBM per device.

v0:
```python
import functools
import math

import jax
import jax.numpy as jnp
from jax import lax
from jax.experimental import pallas as pl
from jax.experimental.pallas import tpu as pltpu
from jax.sharding import PartitionSpec as P

HEADS = 12
SIDE = 7
SHIFT = 3
HEAD_DIM = 32
TABLE = 169
PARAMS = 1771500
CELL = 8
SLOTS = CELL * CELL
GROUP = 4
LANES = GROUP * HEAD_DIM
GROUPS = HEADS // GROUP
FFN_CHUNKS = 3

epsilon = 1e-05
highest = lax.Precision.HIGHEST
f32 = jnp.float32
bf16 = jnp.bfloat16


def from_behind(x, axis, by):
    count = lax.axis_size(axis)
    return lax.ppermute(x, axis, [(i, (i + by) % count) for i in range(count)])


def to_shifted(grid_in):
    lower_rim = from_behind(grid_in[:SHIFT], "ha", -1)
    taller = jnp.concatenate([grid_in[SHIFT:], lower_rim], 0)
    right_rim = from_behind(taller[:, :SHIFT], "wa", -1)
    return jnp.concatenate([taller[:, SHIFT:], right_rim], 1)


def from_shifted(grid_in):
    upper_rim = from_behind(grid_in[-SHIFT:], "ha", 1)
    taller = jnp.concatenate([upper_rim, grid_in[:-SHIFT]], 0)
    left_rim = from_behind(taller[:, -SHIFT:], "wa", 1)
    return jnp.concatenate([left_rim, taller[:, :-SHIFT]], 1)


def to_cells(grid_in, fill):
    rows, cols, channels = grid_in.shape
    split = grid_in.reshape(rows // SIDE, SIDE, cols // SIDE, SIDE, channels)
    extra = CELL - SIDE
    padded = jnp.pad(
        split, ((0, 0), (0, extra), (0, 0), (0, extra), (0, 0)), constant_values=fill
    )
    return padded.transpose(0, 2, 1, 3, 4).reshape(-1, channels)


def from_cells(flat, rows, cols):
    split = flat.reshape(rows // SIDE, cols // SIDE, CELL, CELL, -1)[:, :, :SIDE, :SIDE]
    return split.transpose(0, 2, 1, 3, 4).reshape(rows, cols, -1)


def normalize(values):
    average = jnp.mean(values, -1, keepdims=True)
    centred = values - average
    inverse = lax.rsqrt(jnp.mean(centred * centred, -1, keepdims=True) + epsilon)
    return (centred * inverse, inverse)


def normalize_back(normal_rows, inverse, upstream):
    up_mean = jnp.mean(upstream, -1, keepdims=True)
    cross_mean = jnp.mean(upstream * normal_rows, -1, keepdims=True)
    return inverse * (upstream - up_mean - normal_rows * cross_mean)


def product(left, right, left_dim, right_dim):
    return lax.dot_general(
        left, right, (((left_dim,), (right_dim,)), ((), ())), preferred_element_type=f32
    )


def head_mask():
    shape = (GROUP * SLOTS, LANES)
    row_head = lax.broadcasted_iota(jnp.int32, shape, 0) // SLOTS
    lane_head = lax.broadcasted_iota(jnp.int32, shape, 1) // HEAD_DIM
    return (row_head == lane_head).astype(f32)


def stack_heads(rows, mask):
    return jnp.concatenate([rows] * GROUP, 0) * mask


def gather_heads(stacked, mask):
    kept = stacked * mask
    total = kept[:SLOTS]
    for head in range(1, GROUP):
        total = total + kept[head * SLOTS : (head + 1) * SLOTS]
    return total


def forward_kernel(
    windows, steps, tok_ref, ct_ref, col_ref, row_ref, bias_ref, wq_ref, wp_ref, w1_ref, w2_ref,
    out_ref, mid_ref, qkv_ref, attn_ref, probs_ref, g1_ref, g2_ref, acc1, acc2,
):
    step = pl.program_id(0)

    @pl.when(step == 0)
    def _():
        acc1[...] = jnp.zeros_like(acc1)
        acc2[...] = jnp.zeros_like(acc2)

    channels = tok_ref.shape[1]
    token = tok_ref[...].astype(f32)
    normal, _ = normalize(token)
    qkv_ref[...] = product(normal.astype(bf16), wq_ref[...], 1, 0).astype(bf16)
    mask = head_mask()
    mask_low = mask.astype(bf16)
    for w in range(windows):
        at = slice(w * SLOTS, (w + 1) * SLOTS)
        same = col_ref[at, :] == row_ref[w]
        hidden = jnp.where(same, 0.0, -1e30)
        hidden = jnp.concatenate([hidden] * GROUP, 0)
        for g in range(GROUPS):
            lanes = g * LANES
            query = stack_heads(qkv_ref[at, lanes : lanes + LANES], mask_low)
            key = qkv_ref[at, channels + lanes : channels + lanes + LANES]
            value = qkv_ref[at, 2 * channels + lanes : 2 * channels + lanes + LANES]
            bias = bias_ref[g * GROUP * SLOTS : (g + 1) * GROUP * SLOTS, :]
            scores = product(query, key, 1, 1) * HEAD_DIM ** (-0.5) + bias + hidden
            exponent = jnp.exp(scores - jnp.max(scores, -1, keepdims=True))
            probs = exponent * (1.0 / jnp.sum(exponent, -1, keepdims=True))
            start = (w * GROUPS + g) * GROUP * SLOTS
            probs_ref[start : start + GROUP * SLOTS, :] = probs
            mixed = product(probs.astype(bf16), value, 1, 0)
            attn_ref[at, lanes : lanes + LANES] = gather_heads(mixed, mask).astype(bf16)
    projected = product(attn_ref[...], wp_ref[...], 1, 0).astype(bf16)
    middle = token + projected.astype(f32)
    second, scale = normalize(middle)
    low = second.astype(bf16)
    upstream = ct_ref[...]
    low_turned = low.T
    up_turned = upstream.T
    hidden_units = w1_ref.shape[1]
    width = hidden_units // FFN_CHUNKS
    total = middle
    back = jnp.zeros_like(middle)
    for c in range(FFN_CHUNKS):
        at = slice(c * width, (c + 1) * width)
        w1 = w1_ref[:, at]
        w2 = w2_ref[at, :]
        pre = product(low, w1, 1, 0)
        cdf = 0.5 * (1.0 + lax.erf(pre * 2.0 ** (-0.5)))
        density = jnp.exp(-0.5 * pre * pre) * (2.0 * math.pi) ** (-0.5)
        active = (pre * cdf).astype(bf16)
        total = total + product(active, w2, 1, 0)
        acc2[:, at] += product(up_turned, active, 1, 0)
        grad_pre = (product(upstream, w2, 1, 1) * (cdf + pre * density)).astype(bf16)
        acc1[:, at] += product(low_turned, grad_pre, 1, 0)
        back = back + product(grad_pre, w1, 1, 1)
    out_ref[...] = total.astype(bf16)
    mid_ref[...] = upstream.astype(f32) + normalize_back(second, scale, back)

    @pl.when(step == steps - 1)
    def _():
        g1_ref[...] = acc1[...].astype(bf16)
        g2_ref[...] = acc2[...].T.astype(bf16)


def backward_kernel(
    windows, steps, tok_ref, mid_ref, qkv_ref, attn_ref, probs_ref, wq_ref, wp_ref,
    grad_ref, packed_ref, table_ref, accq, accp, up_ref, gq_ref,
):
    step = pl.program_id(0)

    @pl.when(step == 0)
    def _():
        accq[...] = jnp.zeros_like(accq)
        accp[...] = jnp.zeros_like(accp)
        table_ref[...] = jnp.zeros_like(table_ref)

    channels = tok_ref.shape[1]
    grad_mid = mid_ref[...]
    low = grad_mid.astype(bf16)
    accp[...] += product(attn_ref[...], low, 0, 0)
    up_ref[...] = product(low, wp_ref[...], 1, 1).astype(bf16)
    mask = head_mask()
    mask_low = mask.astype(bf16)
    for w in range(windows):
        at = slice(w * SLOTS, (w + 1) * SLOTS)
        for g in range(GROUPS):
            first = slice(g * LANES, (g + 1) * LANES)
            second = slice(channels + g * LANES, channels + (g + 1) * LANES)
            third = slice(2 * channels + g * LANES, 2 * channels + (g + 1) * LANES)
            rows = slice(g * GROUP * SLOTS, (g + 1) * GROUP * SLOTS)
            query = stack_heads(qkv_ref[at, first], mask_low)
            key = qkv_ref[at, second]
            value = qkv_ref[at, third]
            upstream = stack_heads(up_ref[at, first], mask_low)
            start = (w * GROUPS + g) * GROUP * SLOTS
            probs = probs_ref[start : start + GROUP * SLOTS, :]
            grad_probs = product(upstream, value, 1, 1)
            inner = jnp.sum(probs * grad_probs, -1, keepdims=True)
            grad_scores = probs * (grad_probs - inner)
            table_ref[rows, :] += grad_scores
            scaled = (grad_scores * HEAD_DIM ** (-0.5)).astype(bf16)
            gq_ref[at, first] = gather_heads(product(scaled, key, 1, 0), mask).astype(bf16)
            gq_ref[at, second] = product(scaled, query, 0, 0).astype(bf16)
            gq_ref[at, third] = product(probs.astype(bf16), upstream, 0, 0).astype(bf16)
    normal, scale = normalize(tok_ref[...].astype(f32))
    grads = gq_ref[...]
    accq[...] += product(normal.astype(bf16), grads, 0, 0)
    grad_normed = product(grads, wq_ref[...], 1, 1).astype(bf16).astype(f32)
    grad_ref[...] = (grad_mid + normalize_back(normal, scale, grad_normed)).astype(bf16)

    @pl.when(step == steps - 1)
    def _():
        packed_ref[...] = jnp.zeros_like(packed_ref)
        packed_ref[:channels, : 3 * channels] = accq[...].astype(bf16)
        packed_ref[:channels, 3 * channels :] = accp[...].astype(bf16)


def rows_of(shape, at=0):
    return pl.BlockSpec(shape, lambda i: (i, at))


def whole(shape):
    return pl.BlockSpec(shape, lambda i: (0,) * len(shape))


def local(tokens, cotangent, w_qkv, w_proj, w_fc1, w_fc2, bias_table, rel_index, region):
    tile_rows, tile_cols, channels = tokens.shape
    ffn = w_fc1.shape[1]
    count = (tile_rows // SIDE) * (tile_cols // SIDE)
    windows = math.gcd(count, 4)
    steps = count // windows
    block = windows * SLOTS
    total = count * SLOTS

    both = to_shifted(jnp.concatenate([tokens, cotangent], -1))
    cells = to_cells(both, 0)
    region_cells = to_cells(region[..., None], -1)
    region_rows = region_cells.reshape(count, 1, SLOTS)

    extra = CELL - SIDE
    places = jnp.pad(
        rel_index.reshape(SIDE, SIDE, SIDE, SIDE), ((0, extra),) * 4, constant_values=-1
    ).reshape(1, SLOTS * SLOTS)
    lookup = (jnp.arange(TABLE, dtype=jnp.int32)[:, None] == places).astype(f32)
    pos_bias = lax.dot_general(
        bias_table, lookup, (((0,), (0,)), ((), ())), precision=highest
    ).reshape(HEADS * SLOTS, SLOTS)

    params = pltpu.CompilerParams(
        dimension_semantics=("arbitrary",), vmem_limit_bytes=60 * 1024 * 1024
    )
    shape = jax.ShapeDtypeStruct
    block_cells, grad_mid, qkv, attn, probs, grad_fc1, grad_fc2 = pl.pallas_call(
        functools.partial(forward_kernel, windows, steps),
        name="forward",
        grid=(steps,),
        in_specs=[
            rows_of((block, channels)),
            rows_of((block, channels), 1),
            rows_of((block, 1)),
            pl.BlockSpec((windows, 1, SLOTS), lambda i: (i, 0, 0)),
            whole((HEADS * SLOTS, SLOTS)),
            whole((channels, 3 * channels)),
            whole((channels, channels)),
            whole((channels, ffn)),
            whole((ffn, channels)),
        ],
        out_specs=[
            rows_of((block, channels)),
            rows_of((block, channels)),
            rows_of((block, 3 * channels)),
            rows_of((block, channels)),
            rows_of((windows * HEADS * SLOTS, SLOTS)),
            whole((channels, ffn)),
            whole((ffn, channels)),
        ],
        out_shape=[
            shape((total, channels), bf16),
            shape((total, channels), f32),
            shape((total, 3 * channels), bf16),
            shape((total, channels), bf16),
            shape((count * HEADS * SLOTS, SLOTS), f32),
            shape((channels, ffn), bf16),
            shape((ffn, channels), bf16),
        ],
        scratch_shapes=[pltpu.VMEM((channels, ffn), f32), pltpu.VMEM((channels, ffn), f32)],
        compiler_params=params,
        cost_estimate=pl.CostEstimate(
            flops=20_000_000_000, bytes_accessed=20_000_000, transcendentals=4_000_000
        ),
    )(cells, cells, region_cells, region_rows, pos_bias, w_qkv, w_proj, w_fc1, w_fc2)
    summed_ffn = lax.psum((grad_fc1, grad_fc2), ("ha", "wa"))
    block_out = from_shifted(from_cells(block_cells, tile_rows, tile_cols))

    packed_rows = channels + 16
    grad_cells, packed, bias_grad = pl.pallas_call(
        functools.partial(backward_kernel, windows, steps),
        name="backward",
        grid=(steps,),
        in_specs=[
            rows_of((block, channels)),
            rows_of((block, channels)),
            rows_of((block, 3 * channels)),
            rows_of((block, channels)),
            rows_of((windows * HEADS * SLOTS, SLOTS)),
            whole((channels, 3 * channels)),
            whole((channels, channels)),
        ],
        out_specs=[
            rows_of((block, channels)),
            whole((packed_rows, 4 * channels)),
            whole((HEADS * SLOTS, SLOTS)),
        ],
        out_shape=[
            shape((total, channels), bf16),
            shape((packed_rows, 4 * channels), bf16),
            shape((HEADS * SLOTS, SLOTS), f32),
        ],
        scratch_shapes=[
            pltpu.VMEM((channels, 3 * channels), f32),
            pltpu.VMEM((channels, channels), f32),
            pltpu.VMEM((block, channels), bf16),
            pltpu.VMEM((block, 3 * channels), bf16),
        ],
        compiler_params=params,
        cost_estimate=pl.CostEstimate(
            flops=16_000_000_000, bytes_accessed=16_000_000, transcendentals=1_000_000
        ),
    )(cells, grad_mid, qkv, attn, probs, w_qkv, w_proj)
    grad_table = lax.dot_general(
        bias_grad.reshape(HEADS, SLOTS * SLOTS), lookup, (((1,), (1,)), ((), ())), precision=highest
    )
    packed = lax.dynamic_update_slice(packed, grad_table.astype(bf16), (channels, 0))
    packed, summed_ffn = lax.optimization_barrier((packed, summed_ffn))
    summed = lax.psum(packed, ("ha", "wa")).astype(f32)
    token_grad = from_shifted(from_cells(grad_cells, tile_rows, tile_cols))

    fc1 = summed_ffn[0].astype(f32)
    fc2 = summed_ffn[1].astype(f32)
    norm_sq = jnp.sum(fc1 * fc1) + jnp.sum(fc2 * fc2) + jnp.sum(summed * summed)
    factor = jnp.minimum(1.0, math.sqrt(PARAMS) / (jnp.sqrt(norm_sq) + 1e-06))
    return (
        block_out,
        token_grad,
        summed[:channels, : 3 * channels] * factor,
        summed[:channels, 3 * channels :] * factor,
        fc1 * factor,
        fc2 * factor,
        summed[channels : channels + HEADS, :TABLE].T * factor,
    )


def solution(mesh):
    placed = (P("ha", "wa", None), P("ha", "wa", None), P(), P(), P(), P(), P(), P(), P("ha", "wa"))
    return jax.shard_map(
        local,
        mesh=mesh,
        in_specs=placed,
        out_specs=(P("ha", "wa", None), P("ha", "wa", None), P(), P(), P(), P(), P()),
        check_vma=False,
    )
```

profile of v0, /device:TPU:0, one launch (start us, length us, event | category | flops | bytes accessed | tf_op | source)
XLA Modules:
  0.0 340.1 jit_solution(3399185535853614967)
XLA Ops:
  7.2 1.3 constant_dynamic-update-slice_fusion.1
  8.7 4.0 %collective-permute-start = (bf16[3,28,768]{2,1,0:T(8,128)(2,1)S(1)}, bf16[3,28,768]{2,1,0:T(8,128)(2,1)S(1)}, u32[]{:S(2)}, u32[]{:S(2)}) collective-permute-start(bf16[3,28,768]{2,1,0:T(8,128)(2,1)S(1)} %slice.69), channel_id=1, source_target_pairs={{0,24},{8,0},{16,8},{24,16},{1,25},{9,1},{17,9},{25,17},{2,26},{10... | collective-permute-start | bytes 387080 | tf_op jit(solution)/shard_map/ppermute | solution.py:32
  12.8 0.7 reshape_reshape.3.row_ref
  13.5 1.0 reshape.56.col_ref
  14.9 1.0 convolution_bitcast_fusion
  15.9 0.9 reshape.50.bias_ref
  16.9 2.8 collective-permute-start.1
  19.7 0.4 slice_maximum_fusion
  20.1 2.5 collective-permute-done.1
  22.8 0.4 reshape.46
  23.6 1.3 copy.20
  24.9 26.8 %forward.1 = (bf16[1024,384]{1,0:T(8,128)(2,1)}, f32[1024,384]{1,0:T(8,128)}, bf16[1024,1152]{1,0:T(8,128)(2,1)}, bf16[1024,384]{1,0:T(8,128)(2,1)}, f32[12288,6...) custom-call(bf16[1024,768]{1,0:T(8,128)(2,1)} %bitcast.27, bf16[1024,768]{1,0:T(8,128)(2,1)} %bitcast.28, ...), custom_call_target="tpu_custom_call" | custom-call | flops 20000000000 | bytes 20000000 | tf_op jit(solution)/shard_map/forward/pallas_call | solution.py:258
  51.9 23.3 %backward.1 = (bf16[1024,384]{1,0:T(8,128)(2,1)}, bf16[400,1536]{1,0:T(8,128)(2,1)}, f32[768,64]{1,0:T(8,128)}) custom-call(bf16[1024,768]{1,0:T(8,128)(2,1)} %bitcast.29, f32[1024,384]{1,0:T(8,128)} %get-tuple-element.21.mid_ref, bf16[1024,1152]{1,0:T(8,128)(2,1)} %get-tuple-element.22.qkv_ref, bf16[1024,384]{1,0:T(8,128)(2,1)} %get-tuple-element.23.attn_ref, ...), custom_call_target="tpu_custom_call" | custom-call | flops 16000000000 | bytes 16000000 | tf_op jit(solution)/shard_map/backward/pallas_call | solution.py:301
  75.6 0.8 copy-done.7
  76.8 0.9 collective-permute-start.2
  77.7 1.2 collective-permute-start.4
  79.0 1.4 fusion.5
  80.4 1.5 dynamic_update_slice.3
  82.2 0.7 collective-permute-done.4
  83.0 105.4 %all-reduce.9.cloned.1.call-done = (bf16[384,1536]{1,0:T(8,128)(2,1)}, bf16[1536,384]{1,0:T(8,128)(2,1)}) async-done(((bf16[384,1536]{1,0:T(8,128)(2,1)}, bf16[1536,384]{1,0:T(8,128)(2,1)}), (bf16[384,1536]{1,0:T(8,128)(2,1)}, bf16[1536,384]{1,0:T(8,128)(2,1)})) %all-reduce.9.cloned.1.call-update) | async-done | bytes 2359312 | tf_op jit(solution)/shard_map/psum | solution.py:297
  188.4 1.1 fusion.7
  189.6 1.1 fusion.6
  190.7 1.2 fusion.2
  191.9 1.2 fusion.1
  194.4 129.2 %all-reduce.7.cloned.1.call-done = bf16[400,1536]{1,0:T(8,128)(2,1)} async-done(((bf16[400,1536]{1,0:T(8,128)(2,1)}), bf16[400,1536]{1,0:T(8,128)(2,1)}) %all-reduce.7.cloned.1.call-update) | async-done | bytes 1228816 | tf_op jit(solution)/shard_map/psum | solution.py:340
  323.6 2.5 multiply_reduce_fusion
  326.9 1.6 convert_multiply_fusion
  328.4 1.7 convert_multiply_fusion.2
  330.2 0.3 convert_element_type.16
  330.5 0.6 fusion.8
  331.1 0.9 slice_multiply_fusion.1
  331.9 1.3 slice_multiply_fusion
  (54 shorter events, 2.8 us)
Async XLA Ops:
  7.2 7.7 %copy-start = (f32[169,12]{0,1:T(8,128)S(1)}, f32[169,12]{0,1:T(8,128)}, u32[]{:S(2)}) copy-start(f32[169,12]{0,1:T(8,128)} %param.15) | copy-start | bytes 24340
  7.2 1.3 copy-start.5
  7.2 5.5 %copy-start.10 = (s32[28,28]{1,0:T(8,128)S(1)}, s32[28,28]{1,0:T(8,128)}, u32[]{:S(2)}) copy-start(s32[28,28]{1,0:T(8,128)} %param.17) | copy-start | bytes 9412
  7.2 181.2 %all-reduce.9.cloned.1.call-start = ((), (), s32[]{:S(2)}) async-start(), calls=%async_computation.1 | async-start | bytes 4718592 | tf_op jit(solution)/shard_map/psum | solution.py:297
  8.7 8.1 %collective-permute-start = (bf16[3,28,768]{2,1,0:T(8,128)(2,1)S(1)}, bf16[3,28,768]{2,1,0:T(8,128)(2,1)S(1)}, u32[]{:S(2)}, u32[]{:S(2)}) collective-permute-start(bf16[3,28,768]{2,1,0:T(8,128)(2,1)S(1)} %slice.69), channel_id=1, source_target_pairs={{0,24},{8,0},{16,8},{24,16},{1,25},{9,1},{17,9},{25,17},{2,26},{10... | collective-permute-start | bytes 387080 | tf_op jit(solution)/shard_map/ppermute | solution.py:32
  13.5 1.1 copy-start.9
  16.9 5.7 %collective-permute-start.1 = (bf16[28,3,768]{2,1,0:T(4,128)(2,1)S(1)}, bf16[28,3,768]{2,1,0:T(4,128)(2,1)S(1)}, u32[]{:S(2)}, u32[]{:S(2)}) collective-permute-start(bf16[28,3,768]{2,1,0:T(4,128)(2,1)S(1)} %pad_maximum_fusion.3), channel_id=1, source_target_pairs={{0,7},{1,0},{2,1},{3,2},{4,3},{5,4},{6,5},{7,6},{8,15},{9,8},{10,9... | collective-permute-start | bytes 387080 | tf_op jit(solution)/shard_map/ppermute | solution.py:32
  51.7 271.9 %all-reduce.7.cloned.1.call-start = ((), (), s32[]{:S(2)}) async-start(), calls=%async_computation | async-start | bytes 2457600 | tf_op jit(solution)/shard_map/psum | solution.py:340
  51.9 23.3 %copy-start.6 = (bf16[1024,384]{1,0:T(8,128)(2,1)S(1)}, bf16[1024,384]{1,0:T(8,128)(2,1)}, u32[]{:S(2)}) copy-start(bf16[1024,384]{1,0:T(8,128)(2,1)} %get-tuple-element.20) | copy-start | bytes 2359300
  75.3 1.1 copy-start.7
  76.5 2.3 copy-start.8
  76.8 5.3 %collective-permute-start.2 = (bf16[3,28,384]{2,1,0:T(8,128)(2,1)S(1)}, bf16[3,28,384]{2,1,0:T(8,128)(2,1)S(1)}, u32[]{:S(2)}, u32[]{:S(2)}) collective-permute-start(bf16[3,28,384]{2,1,0:T(8,128)(2,1)S(1)} %slice.73), channel_id=1, source_target_pairs={{0,8},{8,16},{16,24},{24,0},{1,9},{9,17},{17,25},{25,1},{2,10},{10... | collective-permute-start | bytes 193544 | tf_op jit(solution)/shard_map/ppermute | solution.py:32
  77.7 5.3 %collective-permute-start.4 = (bf16[3,28,384]{2,1,0:T(8,128)(2,1)S(1)}, bf16[3,28,384]{2,1,0:T(8,128)(2,1)S(1)}, u32[]{:S(2)}, u32[]{:S(2)}) collective-permute-start(bf16[3,28,384]{2,1,0:T(8,128)(2,1)S(1)} %slice.76), channel_id=1, source_target_pairs={{0,8},{8,16},{16,24},{24,0},{1,9},{9,17},{17,25},{25,1},{2,10},{10... | collective-permute-start | bytes 193544 | tf_op jit(solution)/shard_map/ppermute | solution.py:32
  82.2 106.3 %collective-permute-start.3 = (bf16[28,3,384]{2,1,0:T(4,128)(2,1)S(1)}, bf16[28,3,384]{2,1,0:T(4,128)(2,1)S(1)}, u32[]{:S(2)}, u32[]{:S(2)}) collective-permute-start(bf16[28,3,384]{2,1,0:T(4,128)(2,1)S(1)} %pad_maximum_fusion.5), channel_id=1, source_target_pairs={{0,1},{1,2},{2,3},{3,4},{4,5},{5,6},{6,7},{7,0},{8,9},{9,10},{10,1... | collective-permute-start | bytes 193544 | tf_op jit(solution)/shard_map/ppermute | solution.py:32
  83.0 106.6 %collective-permute-start.5 = (bf16[28,3,384]{2,1,0:T(4,128)(2,1)S(1)}, bf16[28,3,384]{2,1,0:T(4,128)(2,1)S(1)}, u32[]{:S(2)}, u32[]{:S(2)}) collective-permute-start(bf16[28,3,384]{2,1,0:T(4,128)(2,1)S(1)} %pad_maximum_fusion.4), channel_id=1, source_target_pairs={{0,1},{1,2},{2,3},{3,4},{4,5},{5,6},{6,7},{7,0},{8,9},{9,10},{10,1... | collective-permute-start | bytes 193544 | tf_op jit(solution)/shard_map/ppermute | solution.py:32
  188.4 2.3 copy-start.3
  189.6 2.3 copy-start.2
  191.9 134.9 %copy-start.4 = (bf16[1536,384]{1,0:T(8,128)(2,1)S(1)}, bf16[1536,384]{1,0:T(8,128)(2,1)}, u32[]{:S(2)}) copy-start(bf16[1536,384]{1,0:T(8,128)(2,1)} %get-tuple-element.32) | copy-start | bytes 3538948
  328.4 1.7 copy-start.1
Sparse Core Ops, SparseCore 0:
  51.8 136.5 all-reduce.8
  193.8 129.7 all-reduce.6
where the time goes:
time: 340 us
  waiting for transfers between devices  238 us (70%)
  Pallas kernels  50 us (15%)
  between operations  16.4 us (5%)
  other arithmetic  14.3 us (4%)
  local copies, waits for them, and re-layouts  9.7 us (3%)
  starting transfers between devices  9.19 us (3%)
    psum x1, waiting for transfers between devices, local(): summed = lax.psum(packed, ('ha', 'wa')).astype(f32)  129 us
    psum x1, waiting for transfers between devices, local(): summed_ffn = lax.psum((grad_fc1, grad_fc2), ('ha', 'wa'))  105 us
    pallas_call x1, Pallas kernels, local(): pl.pallas_call(functools.partial(forward_kernel, windows, steps), name='f...  26.8 us
    pallas_call x1, Pallas kernels, local(): pl.pallas_call(functools.partial(backward_kernel, windows, steps), name='...  23.3 us
    ppermute x6, starting transfers between devices, from_behind(): return lax.ppermute(x, axis, [(i, (i + by) % count) for i in range(count)])  8.94 us
  transfers between devices with their start and end apart: 8, of which 5 were waited for; matrix products, arithmetic and copies ran while one was open for 4% of the time, Pallas kernels for 7%

commit v1 on v0

--- a/solution.py
+++ b/solution.py
@@ -20,6 +20,11 @@
 LANES = GROUP * HEAD_DIM
 GROUPS = HEADS // GROUP
 FFN_CHUNKS = 3
+SUB = 16
+LANE = 128
+TILE = SUB * LANE
+STREAMS = (4, 2)
+MESH = pl.DeviceIdType.MESH
 
 epsilon = 1e-05
 highest = lax.Precision.HIGHEST
@@ -99,9 +104,183 @@
     return total
 
 
+def to_tiles(values, tiles_ref, at):
+    rows, lanes = values.shape
+    high = rows // SUB
+    low = values.astype(bf16)
+    for column in range(lanes // LANE):
+        block = low[:, column * LANE : (column + 1) * LANE].reshape(high, SUB, LANE)
+        tiles_ref[at + column * high : at + (column + 1) * high] = block
+
+
+def from_tiles(tiles_ref, at, rows, column):
+    high = rows // SUB
+    block = tiles_ref[at + column * high : at + (column + 1) * high]
+    return block.reshape(rows, LANE).astype(f32)
+
+
+def strides_of(size):
+    return [1 << i for i in range(size.bit_length() - 1)]
+
+
+def link_orders(across_ha, across_wa):
+    first, *far = [("wa", stride) for stride in strides_of(across_wa)]
+    near = [("ha", stride) for stride in strides_of(across_ha)]
+    return ([first] + near + far, [first] + near[::-1] + far)
+
+
+def split_streams(group, tiles, devices, parts, orders):
+    units = tiles // devices
+    streams = []
+    base = 0
+    for part in range(parts):
+        size = (units // parts + (part < units % parts)) * devices
+        if size:
+            streams.append((group, base, size, orders[part % len(orders)]))
+        base += size
+    return streams
+
+
+def padded_tiles(tiles, devices):
+    return -(-tiles // devices) * devices
+
+
+def chunk_of(count):
+    return max(size for size in range(1, 17) if count % size == 0)
+
+
+class Exchange:
+    def __init__(self, streams, sources, sums, landing, totals, send_sem, recv_sem):
+        self.streams = streams
+        self.sources, self.sums, self.landing, self.totals = sources, sums, landing, totals
+        self.send_sem, self.recv_sem = send_sem, recv_sem
+        self.rounds = len(streams[0][3])
+        self.copies = []
+        self.places = []
+        for group, base, size, order in streams:
+            places = []
+            low = base
+            for step, (axis, stride) in enumerate(order):
+                half = size >> (step + 1)
+                me = lax.axis_index(axis)
+                bit = (me // stride) % 2
+                partner = {axis: me + stride - 2 * stride * bit}
+                keep = low + bit * half
+                give = low + half - bit * half
+                places.append((partner, keep, give, half))
+                low = keep
+            self.places.append(places)
+
+    def greet(self):
+        barrier = pltpu.get_barrier_semaphore()
+        partners = {link: place[0] for stream, places in zip(self.streams, self.places) for link, place in zip(stream[3], places)}
+        for partner in partners.values():
+            pl.semaphore_signal(barrier, inc=1, device_id=partner, device_id_type=MESH)
+        pl.semaphore_wait(barrier, len(partners))
+
+    def send(self, index, slot, partner, source, target):
+        copy = pltpu.make_async_remote_copy(
+            src_ref=source,
+            dst_ref=target,
+            send_sem=self.send_sem.at[index, slot],
+            recv_sem=self.recv_sem.at[index, slot],
+            device_id=partner,
+            device_id_type=MESH,
+        )
+        copy.start()
+        self.copies.append(copy)
+        return copy
+
+    def halve(self, index, step):
+        group, base, size, _ = self.streams[index]
+        partner, _, give, half = self.places[index][step]
+        source = self.sums[group] if step else self.sources[group]
+        arrive = base + size - (size >> step)
+        return self.send(
+            index, step, partner,
+            source.at[pl.ds(give, half)], self.landing[group].at[pl.ds(arrive, half)],
+        )
+
+    def add(self, index, step):
+        group, base, size, _ = self.streams[index]
+        _, keep, _, half = self.places[index][step]
+        source = self.sums[group] if step else self.sources[group]
+        target = self.sums[group] if step < self.rounds - 1 else self.totals[group]
+        landing = self.landing[group]
+        arrive = base + size - (size >> step)
+        chunk = chunk_of(half)
+
+        def body(i, carry):
+            at = pl.ds(keep + i * chunk, chunk)
+            target[at] = source[at] + landing[pl.ds(arrive + i * chunk, chunk)]
+            return carry
+
+        lax.fori_loop(0, half // chunk, body, 0)
+
+    def double(self, index, step):
+        group = self.streams[index][0]
+        partner, keep, _, half = self.places[index][step]
+        block = self.totals[group].at[pl.ds(keep, half)]
+        return self.send(index, 2 * self.rounds - 1 - step, partner, block, block)
+
+    def run(self):
+        count = len(self.streams)
+        flying = [self.halve(index, 0) for index in range(count)]
+        for step in range(self.rounds):
+            for index in range(count):
+                flying[index].wait_recv()
+                self.add(index, step)
+                if step < self.rounds - 1:
+                    flying[index] = self.halve(index, step + 1)
+                else:
+                    flying[index] = self.double(index, step)
+        for step in reversed(range(self.rounds)):
+            for index in range(count):
+                flying[index].wait_recv()
+                if step:
+                    flying[index] = self.double(index, step - 1)
+        for copy in self.copies:
+            copy.wait_send()
+
+
+def reduce_kernel(
+    streams, ffn_ref, att_ref, ffn_out, att_out, ffn_sum, att_sum, ffn_land, att_land, send_sem, recv_sem
+):
+    exchange = Exchange(
+        streams, (ffn_ref, att_ref), (ffn_sum, att_sum), (ffn_land, att_land), (ffn_out, att_out),
+        send_sem, recv_sem,
+    )
+    exchange.greet()
+    exchange.run()
+
+
+def finish_kernel(ffn_ref, att_ref, gq_ref, gp_ref, g1_ref, g2_ref, table_ref):
+    def squares(ref):
+        chunk = chunk_of(ref.shape[0])
+
+        def body(i, total):
+            block = ref[pl.ds(i * chunk, chunk)].astype(f32)
+            return total + jnp.sum(block * block, 0)
+
+        return lax.fori_loop(0, ref.shape[0] // chunk, body, jnp.zeros((SUB, LANE), f32))
+
+    norm_sq = jnp.sum(squares(ffn_ref) + squares(att_ref))
+    norm_sq = jnp.full((SUB // 2, LANE), norm_sq, f32)
+    factor = jnp.minimum(1.0, math.sqrt(PARAMS) / (jnp.sqrt(norm_sq) + 1e-06))[:1]
+    at = 0
+    for ref, source in ((g1_ref, ffn_ref), (g2_ref, ffn_ref), (gq_ref, att_ref), (gp_ref, att_ref)):
+        at = 0 if ref is gq_ref else at
+        rows, lanes = ref.shape
+        for column in range(lanes // LANE):
+            ref[:, column * LANE : (column + 1) * LANE] = from_tiles(source, at, rows, column) * factor
+        at += ref.size // TILE
+    for column in range(2):
+        table_ref[:, column * LANE : (column + 1) * LANE] = from_tiles(att_ref, at, SUB, column) * factor
+
+
 def forward_kernel(
     windows, steps, tok_ref, ct_ref, col_ref, row_ref, bias_ref, wq_ref, wp_ref, w1_ref, w2_ref,
-    out_ref, mid_ref, qkv_ref, attn_ref, probs_ref, g1_ref, g2_ref, acc1, acc2,
+    out_ref, mid_ref, qkv_ref, attn_ref, probs_ref, tiles_ref, acc1, acc2,
 ):
     step = pl.program_id(0)
 
@@ -163,13 +342,16 @@
 
     @pl.when(step == steps - 1)
     def _():
-        g1_ref[...] = acc1[...].astype(bf16)
-        g2_ref[...] = acc2[...].T.astype(bf16)
+        to_tiles(acc1[...], tiles_ref, 0)
+        to_tiles(acc2[...].T, tiles_ref, acc1.size // TILE)
+        used = (acc1.size + acc2.size) // TILE
+        if used < tiles_ref.shape[0]:
+            tiles_ref[used:] = jnp.zeros((tiles_ref.shape[0] - used, SUB, LANE), bf16)
 
 
 def backward_kernel(
     windows, steps, tok_ref, mid_ref, qkv_ref, attn_ref, probs_ref, wq_ref, wp_ref,
-    grad_ref, packed_ref, table_ref, accq, accp, up_ref, gq_ref,
+    grad_ref, tiles_ref, table_ref, accq, accp, up_ref, gq_ref,
 ):
     step = pl.program_id(0)
 
@@ -215,9 +397,10 @@
 
     @pl.when(step == steps - 1)
     def _():
-        packed_ref[...] = jnp.zeros_like(packed_ref)
-        packed_ref[:channels, : 3 * channels] = accq[...].astype(bf16)
-        packed_ref[:channels, 3 * channels :] = accp[...].astype(bf16)
+        used = (accq.size + accp.size) // TILE
+        to_tiles(accq[...], tiles_ref, 0)
+        to_tiles(accp[...], tiles_ref, accq.size // TILE)
+        tiles_ref[used:] = jnp.zeros((tiles_ref.shape[0] - used, SUB, LANE), bf16)
 
 
 def rows_of(shape, at=0):
@@ -251,11 +434,18 @@
         bias_table, lookup, (((0,), (0,)), ((), ())), precision=highest
     ).reshape(HEADS * SLOTS, SLOTS)
 
+    across = (lax.axis_size("ha"), lax.axis_size("wa"))
+    devices = across[0] * across[1]
+    ffn_tiles = 2 * channels * ffn // TILE
+    att_used = 4 * channels * channels // TILE
+    ffn_padded = padded_tiles(ffn_tiles, devices)
+    att_padded = padded_tiles(att_used + 2, devices)
+
     params = pltpu.CompilerParams(
         dimension_semantics=("arbitrary",), vmem_limit_bytes=60 * 1024 * 1024
     )
     shape = jax.ShapeDtypeStruct
-    block_cells, grad_mid, qkv, attn, probs, grad_fc1, grad_fc2 = pl.pallas_call(
+    block_cells, grad_mid, qkv, attn, probs, ffn_grads = pl.pallas_call(
         functools.partial(forward_kernel, windows, steps),
         name="forward",
         grid=(steps,),
@@ -276,8 +466,7 @@
             rows_of((block, 3 * channels)),
             rows_of((block, channels)),
             rows_of((windows * HEADS * SLOTS, SLOTS)),
-            whole((channels, ffn)),
-            whole((ffn, channels)),
+            whole((ffn_padded, SUB, LANE)),
         ],
         out_shape=[
             shape((total, channels), bf16),
@@ -285,8 +474,7 @@
             shape((total, 3 * channels), bf16),
             shape((total, channels), bf16),
             shape((count * HEADS * SLOTS, SLOTS), f32),
-            shape((channels, ffn), bf16),
-            shape((ffn, channels), bf16),
+            shape((ffn_padded, SUB, LANE), bf16),
         ],
         scratch_shapes=[pltpu.VMEM((channels, ffn), f32), pltpu.VMEM((channels, ffn), f32)],
         compiler_params=params,
@@ -294,11 +482,9 @@
             flops=20_000_000_000, bytes_accessed=20_000_000, transcendentals=4_000_000
         ),
     )(cells, cells, region_cells, region_rows, pos_bias, w_qkv, w_proj, w_fc1, w_fc2)
-    summed_ffn = lax.psum((grad_fc1, grad_fc2), ("ha", "wa"))
     block_out = from_shifted(from_cells(block_cells, tile_rows, tile_cols))
 
-    packed_rows = channels + 16
-    grad_cells, packed, bias_grad = pl.pallas_call(
+    grad_cells, att_grads, bias_grad = pl.pallas_call(
         functools.partial(backward_kernel, windows, steps),
         name="backward",
         grid=(steps,),
@@ -313,12 +499,12 @@
         ],
         out_specs=[
             rows_of((block, channels)),
-            whole((packed_rows, 4 * channels)),
+            whole((att_padded, SUB, LANE)),
             whole((HEADS * SLOTS, SLOTS)),
         ],
         out_shape=[
             shape((total, channels), bf16),
-            shape((packed_rows, 4 * channels), bf16),
+            shape((att_padded, SUB, LANE), bf16),
             shape((HEADS * SLOTS, SLOTS), f32),
         ],
         scratch_shapes=[
@@ -335,24 +521,44 @@
     grad_table = lax.dot_general(
         bias_grad.reshape(HEADS, SLOTS * SLOTS), lookup, (((1,), (1,)), ((), ())), precision=highest
     )
-    packed = lax.dynamic_update_slice(packed, grad_table.astype(bf16), (channels, 0))
-    packed, summed_ffn = lax.optimization_barrier((packed, summed_ffn))
-    summed = lax.psum(packed, ("ha", "wa")).astype(f32)
+    table_tiles = jnp.pad(grad_table, ((0, SUB - HEADS), (0, 2 * LANE - TABLE))).astype(bf16)
+    table_tiles = table_tiles.reshape(SUB, 2, LANE).transpose(1, 0, 2)
+    att_grads = lax.dynamic_update_slice(att_grads, table_tiles, (att_used, 0, 0))
+
+    orders = link_orders(*across)
+    streams = split_streams(0, ffn_padded, devices, STREAMS[0], orders)
+    streams += split_streams(1, att_padded, devices, STREAMS[1], orders)
+    tiled = (shape((ffn_padded, SUB, LANE), bf16), shape((att_padded, SUB, LANE), bf16))
+    in_vmem = pl.BlockSpec(memory_space=pltpu.VMEM)
+    semaphores = pltpu.SemaphoreType.DMA((len(streams), 2 * len(orders[0])))
+    ffn_sum, att_sum = pl.pallas_call(
+        functools.partial(reduce_kernel, streams),
+        name="reduce",
+        out_shape=tiled,
+        in_specs=[in_vmem] * 2,
+        out_specs=[in_vmem] * 2,
+        scratch_shapes=[pltpu.VMEM(part.shape, bf16) for part in tiled] * 2 + [semaphores] * 2,
+        compiler_params=pltpu.CompilerParams(
+            collective_id=0, has_side_effects=True, vmem_limit_bytes=60 * 1024 * 1024
+        ),
+    )(ffn_grads, att_grads)
     token_grad = from_shifted(from_cells(grad_cells, tile_rows, tile_cols))
 
-    fc1 = summed_ffn[0].astype(f32)
-    fc2 = summed_ffn[1].astype(f32)
-    norm_sq = jnp.sum(fc1 * fc1) + jnp.sum(fc2 * fc2) + jnp.sum(summed * summed)
-    factor = jnp.minimum(1.0, math.sqrt(PARAMS) / (jnp.sqrt(norm_sq) + 1e-06))
-    return (
-        block_out,
-        token_grad,
-        summed[:channels, : 3 * channels] * factor,
-        summed[:channels, 3 * channels :] * factor,
-        fc1 * factor,
-        fc2 * factor,
-        summed[channels : channels + HEADS, :TABLE].T * factor,
-    )
+    gq, gp, g1, g2, table = pl.pallas_call(
+        finish_kernel,
+        name="finish",
+        out_shape=[
+            shape((channels, 3 * channels), f32),
+            shape((channels, channels), f32),
+            shape((channels, ffn), f32),
+            shape((ffn, channels), f32),
+            shape((SUB, 2 * LANE), f32),
+        ],
+        in_specs=[in_vmem] * 2,
+        out_specs=[in_vmem] * 5,
+        compiler_params=pltpu.CompilerParams(vmem_limit_bytes=60 * 1024 * 1024),
+    )(ffn_sum, att_sum)
+    return (block_out, token_grad, gq, gp, g1, g2, table[:HEADS, :TABLE].T)
 
 
 def solution(mesh):

time: 340 us -> 148 us (0.44)
  waiting for transfers between devices: 238 us -> 6.95 us
  Pallas kernels: 50 us -> 113 us
  between operations: 16.4 us -> 0.88 us
  other arithmetic: 14.3 us -> 3.02 us
    psum x2 -> x0, waiting for transfers between devices: 235 us -> none  [the longest x1 129 us: local(): summed = lax.psum(packed, ('ha', 'wa')).astype(f32)]
    pallas_call x0 -> x2, Pallas kernels: none -> 62.9 us  [the longest x1 56.9 us: local(): pl.pallas_call(functools.partial(reduce_kernel, streams), name='reduce',...]
    mul x5 -> x0, other arithmetic: 6.08 us -> none  [the longest x1 1.7 us: local(): fc1 * factor]
    reduce_sum x3 -> x0, other arithmetic: 4.93 us -> none  [local(): norm_sq = jnp.sum(fc1 * fc1) + jnp.sum(fc2 * fc2) + jnp.sum(summed * summed)]
    ppermute x6, waiting for transfers between devices: 3.45 us -> 6.95 us  [from_behind(): return lax.ppermute(x, axis, [(i, (i + by) % count) for i in range(count)])]
  transfers between devices with their start and end apart: 8 -> 6, of which waited for: 5 -> 2; matrix products, arithmetic and copies ran while one was open for 4% -> 7% of each run, Pallas kernels for 7% -> 58%
where the time goes in v1:
time: 148 us
  Pallas kernels  113 us (76%)
  local copies, waits for them, and re-layouts  11.5 us (8%)
  starting transfers between devices  10.3 us (7%)
  waiting for transfers between devices  6.95 us (5%)
  other arithmetic  3.02 us (2%)
  matrix products  2.44 us (2%)
    pallas_call x1, Pallas kernels, local(): pl.pallas_call(functools.partial(reduce_kernel, streams), name='reduce',...  56.9 us
    pallas_call x1, Pallas kernels, local(): pl.pallas_call(functools.partial(forward_kernel, windows, steps), name='f...  26.7 us
    pallas_call x1, Pallas kernels, local(): pl.pallas_call(functools.partial(backward_kernel, windows, steps), name='...  23.2 us
    ppermute x6, starting transfers between devices, from_behind(): return lax.ppermute(x, axis, [(i, (i + by) % count) for i in range(count)])  10.3 us
    ppermute x6, waiting for transfers between devices, from_behind(): return lax.ppermute(x, axis, [(i, (i + by) % count) for i in range(count)])  6.95 us
    pallas_call x1, Pallas kernels, local(): pl.pallas_call(finish_kernel, name='finish', out_shape=[shape((channels,...  6.06 us
  transfers between devices with their start and end apart: 6, of which 2 were waited for; matrix products, arithmetic and copies ran while one was open for 7% of the time, Pallas kernels for 58%

profile of v1, /device:TPU:0, one launch (start us, length us, event | category | flops | bytes accessed | tf_op | source)
XLA Modules:
  0.0 148.0 jit_solution(8745336844388679495)
XLA Ops:
  0.7 1.3 constant_dynamic-update-slice_fusion.1
  2.1 4.0 %collective-permute-start = (bf16[3,28,768]{2,1,0:T(8,128)(2,1)S(1)}, bf16[3,28,768]{2,1,0:T(8,128)(2,1)S(1)}, u32[]{:S(2)}, u32[]{:S(2)}) collective-permute-start(bf16[3,28,768]{2,1,0:T(8,128)(2,1)S(1)} %slice.61), channel_id=1, source_target_pairs={{0,24},{8,0},{16,8},{24,16},{1,25},{9,1},{17,9},{25,17},{2,26},{10... | collective-permute-start | bytes 387080 | tf_op jit(solution)/shard_map/ppermute | solution.py:37
  6.2 0.7 reshape_reshape.3.row_ref
  6.9 1.0 reshape.60.col_ref
  8.2 0.1 eq.16
  8.3 1.0 convolution_bitcast_fusion
  9.3 0.9 reshape.53.bias_ref
  10.3 2.8 %collective-permute-start.1 = (bf16[28,3,768]{2,1,0:T(4,128)(2,1)S(1)}, bf16[28,3,768]{2,1,0:T(4,128)(2,1)S(1)}, u32[]{:S(2)}, u32[]{:S(2)}) collective-permute-start(bf16[28,3,768]{2,1,0:T(4,128)(2,1)S(1)} %pad_maximum_fusion.3), channel_id=1, source_target_pairs={{0,7},{1,0},{2,1},{3,2},{4,3},{5,4},{6,5},{7,6},{8,15},{9,8},{10,9... | collective-permute-start | bytes 387080 | tf_op jit(solution)/shard_map/ppermute | solution.py:37
  13.1 0.4 slice_maximum_fusion
  13.5 2.5 %collective-permute-done.1 = bf16[28,3,768]{2,1,0:T(4,128)(2,1)S(1)} collective-permute-done((bf16[28,3,768]{2,1,0:T(4,128)(2,1)S(1)}, bf16[28,3,768]{2,1,0:T(4,128)(2,1)S(1)}, u32[]{:S(2)}, u32[]{:S(2)}) %collective-permute-start.1) | collective-permute-done | bytes 129056 | tf_op jit(solution)/shard_map/ppermute | solution.py:37
  16.1 0.2 pad_maximum_fusion
  16.3 0.4 reshape.49
  16.7 0.3 pad_bitcast_fusion
  17.0 1.3 copy.20
  18.3 26.7 %forward.1 = (bf16[1024,384]{1,0:T(8,128)(2,1)}, f32[1024,384]{1,0:T(8,128)}, bf16[1024,1152]{1,0:T(8,128)(2,1)}, bf16[1024,384]{1,0:T(8,128)(2,1)}, f32[12288,64]{1,0:T(8,128)}, /*index=5*/bf16[576,16,128]{2,1,0:T(8,128)(2,1)}) custom-call(bf16[1024,768]{1,0:T(8,128)(2,1)} %bitcast.38, bf16[1024,768]{1,0:T(8,128)(2,1)} %bitcast.39, ...), custom_call_target="tpu_custom_call" | custom-call | flops 20000000000 | bytes 20000000 | tf_op jit(solution)/shard_map/forward/pallas_call | solution.py:448
  45.1 1.2 copy_bitcast_fusion.1
  46.2 0.2 reshape.55
  46.5 1.0 collective-permute-start.2
  47.5 23.2 %backward.1 = (bf16[1024,384]{1,0:T(8,128)(2,1)}, bf16[320,16,128]{2,1,0:T(8,128)(2,1)}, f32[768,64]{1,0:T(8,128)}) custom-call(bf16[1024,768]{1,0:T(8,128)(2,1)} %bitcast.40, f32[1024,384]{1,0:T(8,128)} %get-tuple-element.24.mid_ref, bf16[1024,1152]{1,0:T(8,128)(2,1)} %get-tuple-element.25.qkv_ref, bf16[1024,384]{1,0:T(8,128)(2,1)} %get-tuple-element.26.attn_ref, ...), custom_call_target="tpu_custom_call" | custom-call | flops 16000000000 | bytes 16000000 | tf_op jit(solution)/shard_map/backward/pallas_call | solution.py:487
  70.7 1.2 copy_bitcast_fusion
  71.9 0.2 reshape.57
  72.1 1.2 collective-permute-start.4
  73.5 1.4 fusion.3
  74.9 0.6 fusion.6.att_ref
  75.5 56.9 %reduce.1 = (bf16[576,16,128]{2,1,0:T(8,128)(2,1)}, bf16[320,16,128]{2,1,0:T(8,128)(2,1)}) custom-call(bf16[576,16,128]{2,1,0:T(8,128)(2,1)} %get-tuple-element.29.ffn_ref, bf16[320,16,128]{2,1,0:T(8,128)(2,1)} %fusion.6.att_ref), custom_call_target="tpu_custom_call" | custom-call | tf_op jit(solution)/shard_map/reduce/pallas_call | solution.py:534
  132.4 6.1 %finish.1 = (f32[384,1152]{1,0:T(8,128)}, f32[384,384]{1,0:T(8,128)}, f32[384,1536]{1,0:T(8,128)}, f32[1536,384]{1,0:T(8,128)}, f32[16,256]{1,0:T(8,128)}) custom-call(bf16[576,16,128]{2,1,0:T(8,128)(2,1)} %get-tuple-element.32.ffn_ref, bf16[320,16,128]{2,1,0:T(8,128)(2,1)} %get-tuple-element.33.att_ref), custom_call_target="tpu_custom_call" | custom-call | tf_op jit(solution)/shard_map/finish/pallas_call | solution.py:547
  138.5 1.3 slice_bitcast_fusion
  140.0 0.5 collective-permute-start.3
  140.6 0.8 collective-permute-start.5
  141.4 4.4 %collective-permute-done.3 = bf16[28,3,384]{2,1,0:T(4,128)(2,1)S(1)} collective-permute-done((bf16[28,3,384]{2,1,0:T(4,128)(2,1)S(1)}, bf16[28,3,384]{2,1,0:T(4,128)(2,1)S(1)}, u32[]{:S(2)}, u32[]{:S(2)}) %collective-permute-start.3) | collective-permute-done | bytes 64544 | tf_op jit(solution)/shard_map/ppermute | solution.py:37
  145.8 1.1 fusion.5
  146.9 1.1 fusion.4
  (30 shorter events, 1.0 us)
Async XLA Ops:
  0.6 7.7 %copy-start = (f32[169,12]{0,1:T(8,128)S(1)}, f32[169,12]{0,1:T(8,128)}, u32[]{:S(2)}) copy-start(f32[169,12]{0,1:T(8,128)} %param.15) | copy-start | bytes 24340
  0.6 1.3 copy-start.1
  0.7 5.5 %copy-start.4 = (s32[28,28]{1,0:T(8,128)S(1)}, s32[28,28]{1,0:T(8,128)}, u32[]{:S(2)}) copy-start(s32[28,28]{1,0:T(8,128)} %param.17) | copy-start | bytes 9412
  2.1 8.1 %collective-permute-start = (bf16[3,28,768]{2,1,0:T(8,128)(2,1)S(1)}, bf16[3,28,768]{2,1,0:T(8,128)(2,1)S(1)}, u32[]{:S(2)}, u32[]{:S(2)}) collective-permute-start(bf16[3,28,768]{2,1,0:T(8,128)(2,1)S(1)} %slice.61), channel_id=1, source_target_pairs={{0,24},{8,0},{16,8},{24,16},{1,25},{9,1},{17,9},{25,17},{2,26},{10... | collective-permute-start | bytes 387080 | tf_op jit(solution)/shard_map/ppermute | solution.py:37
  6.9 1.1 copy-start.3
  10.3 5.7 %collective-permute-start.1 = (bf16[28,3,768]{2,1,0:T(4,128)(2,1)S(1)}, bf16[28,3,768]{2,1,0:T(4,128)(2,1)S(1)}, u32[]{:S(2)}, u32[]{:S(2)}) collective-permute-start(bf16[28,3,768]{2,1,0:T(4,128)(2,1)S(1)} %pad_maximum_fusion.3), channel_id=1, source_target_pairs={{0,7},{1,0},{2,1},{3,2},{4,3},{5,4},{6,5},{7,6},{8,15},{9,8},{10,9... | collective-permute-start | bytes 387080 | tf_op jit(solution)/shard_map/ppermute | solution.py:37
  46.5 93.5 %collective-permute-start.2 = (bf16[3,28,384]{2,1,0:T(8,128)(2,1)S(1)}, bf16[3,28,384]{2,1,0:T(8,128)(2,1)S(1)}, u32[]{:S(2)}, u32[]{:S(2)}) collective-permute-start(bf16[3,28,384]{2,1,0:T(8,128)(2,1)S(1)} %slice.65), channel_id=1, source_target_pairs={{0,8},{8,16},{16,24},{24,0},{1,9},{9,17},{17,25},{25,1},{2,10},{10... | collective-permute-start | bytes 193544 | tf_op jit(solution)/shard_map/ppermute | solution.py:37
  70.7 2.7 %copy-start.2 = (f32[768,64]{1,0:T(8,128)S(1)}, f32[768,64]{1,0:T(8,128)}, u32[]{:S(2)}) copy-start(f32[768,64]{1,0:T(8,128)} %get-tuple-element.31) | copy-start | bytes 589828
  72.1 68.4 %collective-permute-start.4 = (bf16[3,28,384]{2,1,0:T(8,128)(2,1)S(1)}, bf16[3,28,384]{2,1,0:T(8,128)(2,1)S(1)}, u32[]{:S(2)}, u32[]{:S(2)}) collective-permute-start(bf16[3,28,384]{2,1,0:T(8,128)(2,1)S(1)} %slice.68), channel_id=1, source_target_pairs={{0,8},{8,16},{16,24},{24,0},{1,9},{9,17},{17,25},{25,1},{2,10},{10... | collective-permute-start | bytes 193544 | tf_op jit(solution)/shard_map/ppermute | solution.py:37
  140.0 5.8 %collective-permute-start.3 = (bf16[28,3,384]{2,1,0:T(4,128)(2,1)S(1)}, bf16[28,3,384]{2,1,0:T(4,128)(2,1)S(1)}, u32[]{:S(2)}, u32[]{:S(2)}) collective-permute-start(bf16[28,3,384]{2,1,0:T(4,128)(2,1)S(1)} %pad_maximum_fusion.5), channel_id=1, source_target_pairs={{0,1},{1,2},{2,3},{3,4},{4,5},{5,6},{6,7},{7,0},{8,9},{9,10},{10,1... | collective-permute-start | bytes 193544 | tf_op jit(solution)/shard_map/ppermute | solution.py:37
  140.6 6.3 %collective-permute-start.5 = (bf16[28,3,384]{2,1,0:T(4,128)(2,1)S(1)}, bf16[28,3,384]{2,1,0:T(4,128)(2,1)S(1)}, u32[]{:S(2)}, u32[]{:S(2)}) collective-permute-start(bf16[28,3,384]{2,1,0:T(4,128)(2,1)S(1)} %pad_maximum_fusion.4), channel_id=1, source_target_pairs={{0,1},{1,2},{2,3},{3,4},{4,5},{5,6},{6,7},{7,0},{8,9},{9,10},{10,1... | collective-permute-start | bytes 193544 | tf_op jit(solution)/shard_map/ppermute | solution.py:37

commit v2 on v1

v2 whole, which is shorter than its diff:
```python
import functools
import math

import jax
import jax.numpy as jnp
from jax import lax
from jax.experimental import pallas as pl
from jax.experimental.pallas import tpu as pltpu
from jax.sharding import PartitionSpec as P

HEADS = 12
SIDE = 7
SHIFT = 3
HEAD_DIM = 32
TABLE = 169
PARAMS = 1771500
CELL = 8
SLOTS = CELL * CELL
GROUP = 4
LANES = GROUP * HEAD_DIM
GROUPS = HEADS // GROUP
FFN_CHUNKS = 3
SUB = 16
LANE = 128
TILE = SUB * LANE
STREAMS = (4, 2)
PAIR = 2
SLOT_MOVES = ((), (0, 1, 2, 3), (), (0, 1), (2, 3), (0, 1), (2, 3, 0, 1), (2, 3))
MESH = pl.DeviceIdType.MESH

epsilon = 1e-05
highest = lax.Precision.HIGHEST
f32 = jnp.float32
bf16 = jnp.bfloat16


def from_behind(x, axis, by):
    count = lax.axis_size(axis)
    return lax.ppermute(x, axis, [(i, (i + by) % count) for i in range(count)])


def to_shifted(grid_in):
    lower_rim = from_behind(grid_in[:SHIFT], "ha", -1)
    taller = jnp.concatenate([grid_in[SHIFT:], lower_rim], 0)
    right_rim = from_behind(taller[:, :SHIFT], "wa", -1)
    return jnp.concatenate([taller[:, SHIFT:], right_rim], 1)


def from_shifted(grid_in):
    upper_rim = from_behind(grid_in[-SHIFT:], "ha", 1)
    taller = jnp.concatenate([upper_rim, grid_in[:-SHIFT]], 0)
    left_rim = from_behind(taller[:, -SHIFT:], "wa", 1)
    return jnp.concatenate([left_rim, taller[:, :-SHIFT]], 1)


def to_cells(grid_in, fill):
    rows, cols, channels = grid_in.shape
    split = grid_in.reshape(rows // SIDE, SIDE, cols // SIDE, SIDE, channels)
    extra = CELL - SIDE
    padded = jnp.pad(
        split, ((0, 0), (0, extra), (0, 0), (0, extra), (0, 0)), constant_values=fill
    )
    return padded.transpose(0, 2, 1, 3, 4).reshape(-1, channels)


def from_cells(flat, rows, cols):
    split = flat.reshape(rows // SIDE, cols // SIDE, CELL, CELL, -1)[:, :, :SIDE, :SIDE]
    return split.transpose(0, 2, 1, 3, 4).reshape(rows, cols, -1)


def normalize(values):
    average = jnp.mean(values, -1, keepdims=True)
    centred = values - average
    inverse = lax.rsqrt(jnp.mean(centred * centred, -1, keepdims=True) + epsilon)
    return (centred * inverse, inverse)


def normalize_back(normal_rows, inverse, upstream):
    up_mean = jnp.mean(upstream, -1, keepdims=True)
    cross_mean = jnp.mean(upstream * normal_rows, -1, keepdims=True)
    return inverse * (upstream - up_mean - normal_rows * cross_mean)


def product(left, right, left_dim, right_dim):
    return lax.dot_general(
        left, right, (((left_dim,), (right_dim,)), ((), ())), preferred_element_type=f32
    )


def head_mask():
    shape = (GROUP * SLOTS, LANES)
    row_head = lax.broadcasted_iota(jnp.int32, shape, 0) // SLOTS
    lane_head = lax.broadcasted_iota(jnp.int32, shape, 1) // HEAD_DIM
    return (row_head == lane_head).astype(f32)


def stack_heads(rows, mask):
    return jnp.concatenate([rows] * GROUP, 0) * mask


def gather_heads(stacked, mask):
    kept = stacked * mask
    total = kept[:SLOTS]
    for head in range(1, GROUP):
        total = total + kept[head * SLOTS : (head + 1) * SLOTS]
    return total


def to_tiles(values, tiles_ref, at):
    rows, lanes = values.shape
    high = rows // SUB
    low = values.astype(bf16)
    for column in range(lanes // LANE):
        block = low[:, column * LANE : (column + 1) * LANE].reshape(high, SUB, LANE)
        tiles_ref[at + column * high : at + (column + 1) * high] = block


def from_tiles(tiles_ref, at, rows, column):
    high = rows // SUB
    block = tiles_ref[at + column * high : at + (column + 1) * high]
    return block.reshape(rows, LANE).astype(f32)


def strides_of(size):
    return [1 << i for i in range(size.bit_length() - 1)]


def link_orders(across_ha, across_wa):
    first, *far = [("wa", stride) for stride in strides_of(across_wa)]
    near = [("ha", stride) for stride in strides_of(across_ha)]
    return ([first] + near + far, [first] + near[::-1] + far)


def split_streams(group, tiles, devices, parts, orders):
    units = tiles // devices
    streams = []
    base = 0
    for part in range(parts):
        size = (units // parts + (part < units % parts)) * devices
        if size:
            streams.append((group, base, size, orders[part % len(orders)]))
        base += size
    return streams


def padded_tiles(tiles, devices):
    return -(-tiles // devices) * devices


def chunk_of(count):
    return max(size for size in range(1, 17) if count % size == 0)


class Exchange:
    def __init__(self, streams, sources, sums, landing, totals, send_sem, recv_sem):
        self.streams = streams
        self.sources, self.sums, self.landing, self.totals = sources, sums, landing, totals
        self.send_sem, self.recv_sem = send_sem, recv_sem
        self.rounds = len(streams[0][3])
        self.done = [0] * len(streams)
        self.places = []
        for group, base, size, order in streams:
            places = []
            low = base
            for step, (axis, stride) in enumerate(order):
                half = size >> (step + 1)
                me = lax.axis_index(axis)
                bit = (me // stride) % 2
                partner = {axis: me + stride - 2 * stride * bit}
                keep = low + bit * half
                give = low + half - bit * half
                places.append((partner, keep, give, half))
                low = keep
            self.places.append(places)
        self.partners = {
            link: place[0]
            for stream, places in zip(streams, self.places)
            for link, place in zip(stream[3], places)
        }

    def greet(self):
        barrier = pltpu.get_barrier_semaphore()
        for partner in self.partners.values():
            pl.semaphore_signal(barrier, inc=1, device_id=partner, device_id_type=MESH)

    def meet(self):
        pl.semaphore_wait(pltpu.get_barrier_semaphore(), len(self.partners))

    def arrival(self, index, step):
        _, base, size, _ = self.streams[index]
        return base + size - (size >> step)

    def copy(self, index, slot):
        group = self.streams[index][0]
        if slot < self.rounds:
            partner, _, give, half = self.places[index][slot]
            source = (self.sums if slot else self.sources)[group].at[pl.ds(give, half)]
            target = self.landing[group].at[pl.ds(self.arrival(index, slot), half)]
        else:
            partner, keep, _, half = self.places[index][2 * self.rounds - 1 - slot]
            source = self.totals[group].at[pl.ds(keep, half)]
            target = source
        return pltpu.make_async_remote_copy(
            src_ref=source,
            dst_ref=target,
            send_sem=self.send_sem.at[index, slot],
            recv_sem=self.recv_sem.at[index, slot],
            device_id=partner,
            device_id_type=MESH,
        )

    def add(self, index, step):
        group = self.streams[index][0]
        _, keep, _, half = self.places[index][step]
        source = (self.sums if step else self.sources)[group]
        target = (self.sums if step < self.rounds - 1 else self.totals)[group]
        landing = self.landing[group]
        arrive = self.arrival(index, step)
        chunk = chunk_of(half)

        def body(i, carry):
            at = pl.ds(keep + i * chunk, chunk)
            target[at] = source[at] + landing[pl.ds(arrive + i * chunk, chunk)]
            return carry

        lax.fori_loop(0, half // chunk, body, 0)

    def start(self, index):
        self.copy(index, 0).start()

    def advance(self, index):
        slot = self.done[index]
        if slot == 2 * self.rounds:
            return
        self.copy(index, slot).wait_recv()
        if slot < self.rounds:
            self.add(index, slot)
        if slot + 1 < 2 * self.rounds:
            self.copy(index, slot + 1).start()
        self.done[index] = slot + 1

    def drain(self, order):
        while any(self.done[index] < 2 * self.rounds for index in order):
            for index in order:
                self.advance(index)

    def close(self):
        for index in range(len(self.streams)):
            for slot in range(2 * self.rounds):
                self.copy(index, slot).wait_send()


def picks(offset_ref, place):
    labels = lax.broadcasted_iota(jnp.int32, (2 * LANE, LANE), 0)
    return (labels == offset_ref[place : place + 1, :]).astype(f32).astype(bf16)


def fill_bias(offset_ref, label_ref, spread_ref, bias_ref):
    rest = label_ref[...]
    parts = []
    for _ in range(3):
        part = rest.astype(bf16)
        parts.append(part)
        rest = rest - part.astype(f32)
    parts = jnp.concatenate(parts, 0)
    for place in range(CELL):
        spread = product(parts, picks(offset_ref, place), 1, 0)
        spread = spread[:SUB] + (spread[SUB : 2 * SUB] + spread[2 * SUB :])
        spread_ref[pl.ds(place, HEADS, stride=CELL), :] = spread[:HEADS]
    for head in range(HEADS):
        rows = spread_ref[head * CELL : (head + 1) * CELL, :]
        for row in range(CELL):
            at = head * SLOTS + row * CELL
            if row < SIDE:
                turned = pltpu.roll(rows, LANE - (SIDE - row) * CELL, 1)
                bias_ref[at : at + CELL, :] = turned[:, :SLOTS]
            else:
                bias_ref[at : at + CELL, :] = jnp.zeros((CELL, SLOTS), f32)


def gather_offsets(scores_ref, spread_ref, tiles_ref, first):
    for head in range(HEADS):
        total = jnp.zeros((CELL, LANE), f32)
        for row in range(SIDE):
            at = head * SLOTS + row * CELL
            total = total + pltpu.roll(scores_ref[at : at + CELL, :], (SIDE - row) * CELL, 1)
        spread_ref[head * CELL : (head + 1) * CELL, :] = total
    for place in range(CELL):
        rows = spread_ref[pl.ds(place, HEADS, stride=CELL), :]
        rows = jnp.concatenate([rows, jnp.zeros((SUB - HEADS, LANE), f32)], 0)
        tiles_ref[first + place] = rows.astype(bf16)


def block_kernel(
    windows, streams, slots,
    cell_ref, region_ref, offset_ref, label_ref, wq_ref, wp_ref, w1_ref, w2_ref,
    out_ref, grad_ref, early_out, late_out,
    bias_ref, spread_ref, scores_ref, normal_ref, qkv_ref, attn_ref, probs_ref, mid_ref, up_ref, gq_ref,
    acc1, acc2, early_in, late_in, early_sum, late_sum, early_land, late_land, send_sem, recv_sem,
):
    exchange = Exchange(
        streams, (early_in, late_in), (early_sum, late_sum), (early_land, late_land), (early_out, late_out),
        send_sem, recv_sem,
    )
    early = [index for index, stream in enumerate(streams) if stream[0] == 0]
    late = [index for index, stream in enumerate(streams) if stream[0] == 1]
    exchange.greet()
    total_rows, channels = out_ref.shape
    count = total_rows // SLOTS
    block = windows * SLOTS
    hidden_units = w1_ref.shape[1]
    width = hidden_units // FFN_CHUNKS
    stacked_rows = GROUP * SLOTS
    mask = head_mask()
    mask_low = mask.astype(bf16)
    fill_bias(offset_ref, label_ref, spread_ref, bias_ref)
    acc1[...] = jnp.zeros_like(acc1)
    acc2[...] = jnp.zeros_like(acc2)

    def forward(step, carry):
        rows = pl.ds(pl.multiple_of(step * block, block), block)
        token = cell_ref[rows, :channels].astype(f32)
        upstream = cell_ref[rows, channels:]
        normal, _ = normalize(token)
        normal_low = normal.astype(bf16)
        normal_ref[rows, :] = normal_low
        qkv_ref[rows, :] = product(normal_low, wq_ref[...], 1, 0).astype(bf16)
        for w in range(windows):
            at = pl.ds(pl.multiple_of(step * block + w * SLOTS, SLOTS), SLOTS)
            labels = jnp.broadcast_to(region_ref[step * windows + w], (SLOTS, SLOTS))
            hidden = jnp.where(labels == labels.T, 0.0, -1e30)
            hidden = jnp.concatenate([hidden] * GROUP, 0)
            for g in range(GROUPS):
                lanes = g * LANES
                query = stack_heads(qkv_ref[at, lanes : lanes + LANES], mask_low)
                key = qkv_ref[at, channels + lanes : channels + lanes + LANES]
                value = qkv_ref[at, 2 * channels + lanes : 2 * channels + lanes + LANES]
                bias = bias_ref[g * stacked_rows : (g + 1) * stacked_rows, :]
                scores = product(query, key, 1, 1) * HEAD_DIM ** (-0.5) + bias + hidden
                exponent = jnp.exp(scores - jnp.max(scores, -1, keepdims=True))
                probs = (exponent * (1.0 / jnp.sum(exponent, -1, keepdims=True))).astype(bf16)
                start = ((step * windows + w) * GROUPS + g) * stacked_rows
                probs_ref[pl.ds(pl.multiple_of(start, stacked_rows), stacked_rows), :] = probs
                mixed = product(probs, value, 1, 0)
                attn_ref[at, lanes : lanes + LANES] = gather_heads(mixed, mask).astype(bf16)
        projected = product(attn_ref[rows, :], wp_ref[...], 1, 0).astype(bf16)
        middle = token + projected.astype(f32)
        second, scale = normalize(middle)
        low = second.astype(bf16)
        low_turned = low.T
        up_turned = upstream.T
        total = middle
        back = jnp.zeros_like(middle)
        for c in range(FFN_CHUNKS):
            at = slice(c * width, (c + 1) * width)
            w1 = w1_ref[:, at]
            w2 = w2_ref[at, :]
            pre = product(low, w1, 1, 0)
            cdf = 0.5 * (1.0 + lax.erf(pre * 2.0 ** (-0.5)))
            density = jnp.exp(-0.5 * pre * pre) * (2.0 * math.pi) ** (-0.5)
            active = (pre * cdf).astype(bf16)
            total = total + product(active, w2, 1, 0)
            acc2[:, at] += product(up_turned, active, 1, 0)
            grad_pre = (product(upstream, w2, 1, 1) * (cdf + pre * density)).astype(bf16)
            acc1[:, at] += product(low_turned, grad_pre, 1, 0)
            back = back + product(grad_pre, w1, 1, 1)
        out_ref[rows, :] = total.astype(bf16)
        mid_ref[rows, :] = upstream.astype(f32) + normalize_back(second, scale, back)
        return carry

    lax.fori_loop(0, count // windows, forward, 0)

    mid_low = mid_ref[...].astype(bf16)
    to_tiles(acc1[...], early_in, 0)
    to_tiles(acc2[...].T, early_in, acc1.size // TILE)
    used = 2 * acc1.size // TILE
    to_tiles(product(attn_ref[...], mid_low, 0, 0), early_in, used)
    used += channels * channels // TILE
    if used < early_in.shape[0]:
        early_in[used:] = jnp.zeros((early_in.shape[0] - used, SUB, LANE), bf16)
    exchange.meet()
    for index in early:
        exchange.start(index)
    up_ref[...] = product(mid_low, wp_ref[...], 1, 1).astype(bf16)
    scores_ref[...] = jnp.zeros_like(scores_ref)

    def backward(step, carry):
        for slot, moves in enumerate(slots):
            if moves:
                @pl.when(step == slot)
                def _(moves=moves):
                    for index in moves:
                        exchange.advance(index)

        for w in range(PAIR):
            at = pl.ds(pl.multiple_of((step * PAIR + w) * SLOTS, SLOTS), SLOTS)
            for g in range(GROUPS):
                first = slice(g * LANES, (g + 1) * LANES)
                second = slice(channels + g * LANES, channels + (g + 1) * LANES)
                third = slice(2 * channels + g * LANES, 2 * channels + (g + 1) * LANES)
                rows = slice(g * stacked_rows, (g + 1) * stacked_rows)
                query = stack_heads(qkv_ref[at, first], mask_low)
                key = qkv_ref[at, second]
                value = qkv_ref[at, third]
                upstream = stack_heads(up_ref[at, first], mask_low)
                start = ((step * PAIR + w) * GROUPS + g) * stacked_rows
                low = probs_ref[pl.ds(pl.multiple_of(start, stacked_rows), stacked_rows), :]
                probs = low.astype(f32)
                grad_probs = product(upstream, value, 1, 1)
                inner = jnp.sum(probs * grad_probs, -1, keepdims=True)
                grad_scores = probs * (grad_probs - inner)
                scores_ref[rows, :SLOTS] += grad_scores
                scaled = (grad_scores * HEAD_DIM ** (-0.5)).astype(bf16)
                gq_ref[at, first] = gather_heads(product(scaled, key, 1, 0), mask).astype(bf16)
                gq_ref[at, second] = product(scaled, query, 0, 0).astype(bf16)
                gq_ref[at, third] = product(low, upstream, 0, 0).astype(bf16)
        return carry

    lax.fori_loop(0, count // PAIR, backward, 0)

    normal_turned = normal_ref[...].T
    to_tiles(product(normal_turned, gq_ref[...], 1, 0), late_in, 0)
    used = 3 * channels * channels // TILE
    gather_offsets(scores_ref, spread_ref, late_in, used)
    used += CELL
    if used < late_in.shape[0]:
        late_in[used:] = jnp.zeros((late_in.shape[0] - used, SUB, LANE), bf16)
    for index in late:
        exchange.start(index)

    def finish_tokens(step, carry):
        rows = pl.ds(pl.multiple_of(step * block, block), block)
        normal, scale = normalize(cell_ref[rows, :channels].astype(f32))
        grad_normed = product(gq_ref[rows, :], wq_ref[...], 1, 1).astype(bf16).astype(f32)
        grad_ref[rows, :] = (mid_ref[rows, :] + normalize_back(normal, scale, grad_normed)).astype(bf16)
        return carry

    lax.fori_loop(0, count // windows, finish_tokens, 0)
    exchange.drain(late + early)
    exchange.close()


def finish_kernel(early_ref, late_ref, offset_ref, gq_ref, gp_ref, g1_ref, g2_ref, table_ref):
    def squares(ref, first, last):
        chunk = chunk_of(last - first)

        def body(i, total):
            block = ref[pl.ds(first + i * chunk, chunk)].astype(f32)
            return total + jnp.sum(block * block, 0)

        return lax.fori_loop(0, (last - first) // chunk, body, jnp.zeros((SUB, LANE), f32))

    used = gq_ref.size // TILE
    table = jnp.zeros((SUB, 2 * LANE), f32)
    for place in range(CELL):
        table = table + product(late_ref[used + place], picks(offset_ref, place), 1, 1)
    norm_sq = jnp.sum(squares(early_ref, 0, early_ref.shape[0]) + squares(late_ref, 0, used))
    norm_sq = norm_sq + jnp.sum(table * table)
    norm_sq = jnp.full((SUB // 2, LANE), norm_sq, f32)
    factor = jnp.minimum(1.0, math.sqrt(PARAMS) / (jnp.sqrt(norm_sq) + 1e-06))[:1]
    at = 0
    for ref, source in ((g1_ref, early_ref), (g2_ref, early_ref), (gp_ref, early_ref), (gq_ref, late_ref)):
        at = 0 if ref is gq_ref else at
        rows, lanes = ref.shape
        for column in range(lanes // LANE):
            ref[:, column * LANE : (column + 1) * LANE] = from_tiles(source, at, rows, column) * factor
        at += ref.size // TILE
    for column in range(2):
        lanes = slice(column * LANE, (column + 1) * LANE)
        table_ref[:, lanes] = table[:, lanes] * factor


def offsets_of(rel_index):
    rel = rel_index.reshape(SIDE, SIDE, SIDE, SIDE)
    behind = rel[1:, :, 0][::-1]
    ahead = rel[0].transpose(1, 0, 2)
    places = jnp.concatenate([behind, ahead], 0).transpose(1, 0, 2)
    places = jnp.pad(places, ((0, 1), (1, 2), (0, 1)), constant_values=-1)
    return places.reshape(CELL, LANE)


def local(tokens, cotangent, w_qkv, w_proj, w_fc1, w_fc2, bias_table, rel_index, region):
    tile_rows, tile_cols, channels = tokens.shape
    ffn = w_fc1.shape[1]
    count = (tile_rows // SIDE) * (tile_cols // SIDE)
    windows = math.gcd(count, 4)
    total = count * SLOTS

    both = to_shifted(jnp.concatenate([tokens, cotangent], -1))
    cells = to_cells(both, 0)
    labels = to_cells(region[..., None], -1).astype(f32).reshape(count, 1, SLOTS)
    offsets = offsets_of(rel_index)
    label_rows = jnp.pad(bias_table.T, ((0, SUB - HEADS), (0, 2 * LANE - TABLE)))

    across = (lax.axis_size("ha"), lax.axis_size("wa"))
    devices = across[0] * across[1]
    early_tiles = padded_tiles((2 * channels * ffn + channels * channels) // TILE, devices)
    late_tiles = padded_tiles(3 * channels * channels // TILE + CELL, devices)
    orders = link_orders(*across)
    streams = split_streams(0, early_tiles, devices, STREAMS[0], orders)
    early_count = len(streams)
    streams += split_streams(1, late_tiles, devices, STREAMS[1], orders)
    slots = [[index for index in moves if index < early_count] for moves in SLOT_MOVES[: count // PAIR]]

    shape = jax.ShapeDtypeStruct
    early = (early_tiles, SUB, LANE)
    late = (late_tiles, SUB, LANE)
    in_vmem = pl.BlockSpec(memory_space=pltpu.VMEM)
    semaphores = pltpu.SemaphoreType.DMA((len(streams), 2 * len(orders[0])))
    vmem_limit = 62 * 1024 * 1024
    block_cells, grad_cells, early_sum, late_sum = pl.pallas_call(
        functools.partial(block_kernel, windows, streams, slots),
        name="block",
        out_shape=[
            shape((total, channels), bf16), shape((total, channels), bf16), shape(early, bf16), shape(late, bf16),
        ],
        in_specs=[in_vmem] * 8,
        out_specs=[in_vmem] * 4,
        scratch_shapes=[
            pltpu.VMEM((HEADS * SLOTS, SLOTS), f32),
            pltpu.VMEM((HEADS * CELL, LANE), f32),
            pltpu.VMEM((HEADS * SLOTS, LANE), f32),
            pltpu.VMEM((total, channels), bf16),
            pltpu.VMEM((total, 3 * channels), bf16),
            pltpu.VMEM((total, channels), bf16),
            pltpu.VMEM((count * HEADS * SLOTS, SLOTS), bf16),
            pltpu.VMEM((total, channels), f32),
            pltpu.VMEM((total, channels), bf16),
            pltpu.VMEM((total, 3 * channels), bf16),
            pltpu.VMEM((channels, ffn), f32),
            pltpu.VMEM((channels, ffn), f32),
        ] + [pltpu.VMEM(group, bf16) for group in (early, late)] * 3 + [semaphores] * 2,
        compiler_params=pltpu.CompilerParams(
            collective_id=0, has_side_effects=True, vmem_limit_bytes=vmem_limit
        ),
        cost_estimate=pl.CostEstimate(
            flops=36_000_000_000, bytes_accessed=20_000_000, transcendentals=5_000_000
        ),
    )(cells, labels, offsets, label_rows, w_qkv, w_proj, w_fc1, w_fc2)
    block_out = from_shifted(from_cells(block_cells, tile_rows, tile_cols))
    token_grad = from_shifted(from_cells(grad_cells, tile_rows, tile_cols))

    gq, gp, g1, g2, table = pl.pallas_call(
        finish_kernel,
        name="finish",
        out_shape=[
            shape((channels, 3 * channels), f32),
            shape((channels, channels), f32),
            shape((channels, ffn), f32),
            shape((ffn, channels), f32),
            shape((SUB, 2 * LANE), f32),
        ],
        in_specs=[in_vmem] * 3,
        out_specs=[in_vmem] * 5,
        compiler_params=pltpu.CompilerParams(vmem_limit_bytes=vmem_limit),
    )(early_sum, late_sum, offsets)
    return (block_out, token_grad, gq, gp, g1, g2, table[:HEADS, :TABLE].T)


def solution(mesh):
    placed = (P("ha", "wa", None), P("ha", "wa", None), P(), P(), P(), P(), P(), P(), P("ha", "wa"))
    return jax.shard_map(
        local,
        mesh=mesh,
        in_specs=placed,
        out_specs=(P("ha", "wa", None), P("ha", "wa", None), P(), P(), P(), P(), P()),
        check_vma=False,
    )
```

time: 148 us -> 129 us (0.87)
  Pallas kernels: 113 us -> 97 us
  matrix products: 2.44 us -> 0 us
  local copies, waits for them, and re-layouts: 11.5 us -> 9.51 us
    pallas_call x3 -> x1, Pallas kernels: 107 us -> 90.7 us  [local(): pl.pallas_call(functools.partial(block_kernel, windows, streams, slots),...]
    dot_general x2 -> x0, matrix products: 2.44 us -> none  [the longest x1 1.41 us: local(): lax.dot_general(bias_grad.reshape(HEADS, SLOTS * SLOTS), lookup, (((1,),...]
  transfers between devices with their start and end apart: 6 -> 6, of which waited for: 2 -> 3; matrix products, arithmetic and copies ran while one was open for 7% -> 4% of each run, Pallas kernels for 58% -> 5%
where the time goes in v2:
time: 129 us; the launch traced here: 128 us
  Pallas kernels  97 us (75%)
  starting transfers between devices  9.6 us (7%)
  local copies, waits for them, and re-layouts  9.51 us (7%)
  waiting for transfers between devices  8.17 us (6%)
  other arithmetic  3.05 us (2%)
    pallas_call x1, Pallas kernels, local(): pl.pallas_call(functools.partial(block_kernel, windows, streams, slots),...  90.7 us
    ppermute x6, starting transfers between devices, from_behind(): return lax.ppermute(x, axis, [(i, (i + by) % count) for i in range(count)])  9.6 us
    ppermute x6, waiting for transfers between devices, from_behind(): return lax.ppermute(x, axis, [(i, (i + by) % count) for i in range(count)])  8.17 us
    pallas_call x1, Pallas kernels, local(): pl.pallas_call(finish_kernel, name='finish', out_shape=[shape((channels,...  6.36 us
  transfers between devices with their start and end apart: 6, of which 3 were waited for; matrix products, arithmetic and copies ran while one was open for 4% of the time, Pallas kernels for 5%

profile of v2, /device:TPU:0, one launch (start us, length us, event | category | flops | bytes accessed | tf_op | source)
XLA Modules:
  0.0 128.3 jit_solution(10189616582788009665)
XLA Ops:
  0.7 1.3 constant_dynamic-update-slice_fusion.1
  2.0 0.1 constant_dynamic-update-slice_fusion
  2.1 4.0 %collective-permute-start = (bf16[3,28,768]{2,1,0:T(8,128)(2,1)S(1)}, bf16[3,28,768]{2,1,0:T(8,128)(2,1)S(1)}, u32[]{:S(2)}, u32[]{:S(2)}) collective-permute-start(bf16[3,28,768]{2,1,0:T(8,128)(2,1)S(1)} %slice.70), channel_id=1, source_target_pairs={{0,24},{8,0},{16,8},{24,16},{1,25},{9,1},{17,9},{25,17},{2,26},{10... | collective-permute-start | bytes 387080 | tf_op jit(solution)/shard_map/ppermute | solution.py:39
  6.1 0.1 reshape_broadcast_in_dim.3
  6.3 0.1 reshape.58
  6.4 0.1 slice.69
  6.5 0.5 slice-done
  6.9 0.1 squeeze.7
  7.0 0.7 convert_element_type.24.region_ref
  7.8 0.7 reshape.59.offset_ref
  8.5 0.6 pad.19.label_ref
  9.1 0.1 collective-permute-done
  9.3 2.7 %collective-permute-start.1 = (bf16[28,3,768]{2,1,0:T(4,128)(2,1)S(1)}, bf16[28,3,768]{2,1,0:T(4,128)(2,1)S(1)}, u32[]{:S(2)}, u32[]{:S(2)}) collective-permute-start(bf16[28,3,768]{2,1,0:T(4,128)(2,1)S(1)} %pad_maximum_fusion.3), channel_id=1, source_target_pairs={{0,7},{1,0},{2,1},{3,2},{4,3},{5,4},{6,5},{7,6},{8,15},{9,8},{10,9... | collective-permute-start | bytes 387080 | tf_op jit(solution)/shard_map/ppermute | solution.py:39
  12.0 0.4 slice_maximum_fusion
  12.3 2.5 %collective-permute-done.1 = bf16[28,3,768]{2,1,0:T(4,128)(2,1)S(1)} collective-permute-done((bf16[28,3,768]{2,1,0:T(4,128)(2,1)S(1)}, bf16[28,3,768]{2,1,0:T(4,128)(2,1)S(1)}, u32[]{:S(2)}, u32[]{:S(2)}) %collective-permute-start.1) | collective-permute-done | bytes 129056 | tf_op jit(solution)/shard_map/ppermute | solution.py:39
  14.9 0.2 pad_maximum_fusion
  15.1 0.4 reshape.56
  15.5 0.3 pad_bitcast_fusion
  15.8 1.3 %copy.21 = bf16[4,4,8,8,768]{4,3,2,1,0:T(8,128)(2,1)} copy(bf16[4,4,8,8,768]{4,3,1,2,0:T(8,128)(2,1)S(1)} %pad_bitcast_fusion) | data formatting | bytes 3145728 | tf_op jit(solution)/shard_map/transpose | solution.py:63
  17.1 90.7 %block.1 = (bf16[1024,384]{1,0:T(8,128)(2,1)}, bf16[1024,384]{1,0:T(8,128)(2,1)}, bf16[672,16,128]{2,1,0:T(8,128)(2,1)}, bf16[224,16,128]{2,1,0:T(8,128)(2,1)}) custom-call(bf16[1024,768]{1,0:T(8,128)(2,1)} %bitcast.24, f32[16,1,64]{2,1,0:T(1,128)} %convert_element_type.24.region_ref, s32[8,128]{1,0:T(8,128)} %reshape.59.offset_ref, ...), custom_call_target="tpu_custom_call" | custom-call | flops 35999997952 | bytes 20000000 | tf_op jit(solution)/shard_map/block/pallas_call | solution.py:511
  107.8 1.2 copy_bitcast_fusion.1
  109.1 0.2 reshape.61
  109.3 0.1 copy_bitcast_fusion
  109.4 0.2 reshape.63
  109.6 0.8 collective-permute-start.2
  110.4 1.9 %collective-permute-start.4 = (bf16[3,28,384]{2,1,0:T(8,128)(2,1)S(1)}, bf16[3,28,384]{2,1,0:T(8,128)(2,1)S(1)}, u32[]{:S(2)}, u32[]{:S(2)}) collective-permute-start(bf16[3,28,384]{2,1,0:T(8,128)(2,1)S(1)} %slice.78), channel_id=1, source_target_pairs={{0,8},{8,16},{16,24},{24,0},{1,9},{9,17},{17,25},{25,1},{2,10},{10... | collective-permute-start | bytes 193544 | tf_op jit(solution)/shard_map/ppermute | solution.py:39
  112.4 6.4 %finish.1 = (f32[384,1152]{1,0:T(8,128)}, f32[384,384]{1,0:T(8,128)}, f32[384,1536]{1,0:T(8,128)}, f32[1536,384]{1,0:T(8,128)}, f32[16,256]{1,0:T(8,128)}) custom-call(bf16[672,16,128]{2,1,0:T(8,128)(2,1)} %get-tuple-element.18.early_ref, bf16[224,16,128]{2,1,0:T(8,128)(2,1)} %get-tuple-element.19.late_ref, s32[8,128]{1,0:T(8,128)} %reshape.59.offset_ref), custom_call_target="tpu_custom_call" | custom-call | tf_op jit(solution)/shard_map/finish/pallas_call | solution.py:543
  118.7 1.3 %slice_bitcast_fusion = f32[169,12]{0,1:T(8,128)} fusion(f32[16,256]{1,0:T(8,128)} %get-tuple-element.24), kind=kLoop, calls=%fused_computation.15 | loop fusion | bytes 16224 | tf_op jit(solution)/shard_map/transpose | solution.py:557
  120.4 0.1 collective-permute-start.5
  120.5 5.5 %collective-permute-done.3 = bf16[28,3,384]{2,1,0:T(4,128)(2,1)S(1)} collective-permute-done((bf16[28,3,384]{2,1,0:T(4,128)(2,1)S(1)}, bf16[28,3,384]{2,1,0:T(4,128)(2,1)S(1)}, u32[]{:S(2)}, u32[]{:S(2)}) %collective-permute-start.3) | collective-permute-done | bytes 64544 | tf_op jit(solution)/shard_map/ppermute | solution.py:39
  126.0 1.1 fusion.1
  127.2 1.1 fusion
  (30 shorter events, 0.5 us)
Async XLA Ops:
  0.6 1.3 %copy-start = (bf16[28,28,384]{2,1,0:T(8,128)(2,1)S(1)}, bf16[28,28,384]{2,1,0:T(8,128)(2,1)}, u32[]{:S(2)}) copy-start(bf16[28,28,384]{2,1,0:T(8,128)(2,1)} %param.10) | copy-start | bytes 1806340
  0.6 5.5 %copy-start.4 = (s32[28,28]{1,0:T(8,128)S(1)}, s32[28,28]{1,0:T(8,128)}, u32[]{:S(2)}) copy-start(s32[28,28]{1,0:T(8,128)} %param.17) | copy-start | bytes 9412
  0.7 5.6 %copy-start.2 = (s32[49,49]{1,0:T(8,128)S(1)}, s32[49,49]{1,0:T(8,128)}, u32[]{:S(2)}) copy-start(s32[49,49]{1,0:T(8,128)} %param.16) | copy-start | bytes 28816
  2.1 7.1 %collective-permute-start = (bf16[3,28,768]{2,1,0:T(8,128)(2,1)S(1)}, bf16[3,28,768]{2,1,0:T(8,128)(2,1)S(1)}, u32[]{:S(2)}, u32[]{:S(2)}) collective-permute-start(bf16[3,28,768]{2,1,0:T(8,128)(2,1)S(1)} %slice.70), channel_id=1, source_target_pairs={{0,24},{8,0},{16,8},{24,16},{1,25},{9,1},{17,9},{25,17},{2,26},{10... | collective-permute-start | bytes 387080 | tf_op jit(solution)/shard_map/ppermute | solution.py:39
  6.2 0.7 slice-start
  6.4 2.1 %copy-start.3 = (f32[169,12]{0,1:T(8,128)S(1)}, f32[169,12]{0,1:T(8,128)}, u32[]{:S(2)}) copy-start(f32[169,12]{0,1:T(8,128)} %param.15) | copy-start | bytes 24340
  9.3 5.6 %collective-permute-start.1 = (bf16[28,3,768]{2,1,0:T(4,128)(2,1)S(1)}, bf16[28,3,768]{2,1,0:T(4,128)(2,1)S(1)}, u32[]{:S(2)}, u32[]{:S(2)}) collective-permute-start(bf16[28,3,768]{2,1,0:T(4,128)(2,1)S(1)} %pad_maximum_fusion.3), channel_id=1, source_target_pairs={{0,7},{1,0},{2,1},{3,2},{4,3},{5,4},{6,5},{7,6},{8,15},{9,8},{10,9... | collective-permute-start | bytes 387080 | tf_op jit(solution)/shard_map/ppermute | solution.py:39
  107.8 1.5 %copy-start.1 = (bf16[1024,384]{1,0:T(8,128)(2,1)S(1)}, bf16[1024,384]{1,0:T(8,128)(2,1)}, u32[]{:S(2)}) copy-start(bf16[1024,384]{1,0:T(8,128)(2,1)} %get-tuple-element.17) | copy-start | bytes 2359300
  109.6 10.6 %collective-permute-start.2 = (bf16[3,28,384]{2,1,0:T(8,128)(2,1)S(1)}, bf16[3,28,384]{2,1,0:T(8,128)(2,1)S(1)}, u32[]{:S(2)}, u32[]{:S(2)}) collective-permute-start(bf16[3,28,384]{2,1,0:T(8,128)(2,1)S(1)} %slice.75), channel_id=1, source_target_pairs={{0,8},{8,16},{16,24},{24,0},{1,9},{9,17},{17,25},{25,1},{2,10},{10... | collective-permute-start | bytes 193544 | tf_op jit(solution)/shard_map/ppermute | solution.py:39
  110.4 9.9 %collective-permute-start.4 = (bf16[3,28,384]{2,1,0:T(8,128)(2,1)S(1)}, bf16[3,28,384]{2,1,0:T(8,128)(2,1)S(1)}, u32[]{:S(2)}, u32[]{:S(2)}) collective-permute-start(bf16[3,28,384]{2,1,0:T(8,128)(2,1)S(1)} %slice.78), channel_id=1, source_target_pairs={{0,8},{8,16},{16,24},{24,0},{1,9},{9,17},{17,25},{25,1},{2,10},{10... | collective-permute-start | bytes 193544 | tf_op jit(solution)/shard_map/ppermute | solution.py:39
  120.3 5.8 %collective-permute-start.3 = (bf16[28,3,384]{2,1,0:T(4,128)(2,1)S(1)}, bf16[28,3,384]{2,1,0:T(4,128)(2,1)S(1)}, u32[]{:S(2)}, u32[]{:S(2)}) collective-permute-start(bf16[28,3,384]{2,1,0:T(4,128)(2,1)S(1)} %pad_maximum_fusion.5), channel_id=1, source_target_pairs={{0,1},{1,2},{2,3},{3,4},{4,5},{5,6},{6,7},{7,0},{8,9},{9,10},{10,1... | collective-permute-start | bytes 193544 | tf_op jit(solution)/shard_map/ppermute | solution.py:39
  120.4 6.8 %collective-permute-start.5 = (bf16[28,3,384]{2,1,0:T(4,128)(2,1)S(1)}, bf16[28,3,384]{2,1,0:T(4,128)(2,1)S(1)}, u32[]{:S(2)}, u32[]{:S(2)}) collective-permute-start(bf16[28,3,384]{2,1,0:T(4,128)(2,1)S(1)} %pad_maximum_fusion.4), channel_id=1, source_target_pairs={{0,1},{1,2},{2,3},{3,4},{4,5},{5,6},{6,7},{7,0},{8,9},{9,10},{10,1... | collective-permute-start | bytes 193544 | tf_op jit(solution)/shard_map/ppermute | solution.py:39

commit v3 on v2

--- a/solution.py
+++ b/solution.py
@@ -27,45 +27,12 @@
 PAIR = 2
 SLOT_MOVES = ((), (0, 1, 2, 3), (), (0, 1), (2, 3), (0, 1), (2, 3, 0, 1), (2, 3))
 MESH = pl.DeviceIdType.MESH
+PITCH = 32
 
 epsilon = 1e-05
 highest = lax.Precision.HIGHEST
 f32 = jnp.float32
 bf16 = jnp.bfloat16
-
-
-def from_behind(x, axis, by):
-    count = lax.axis_size(axis)
-    return lax.ppermute(x, axis, [(i, (i + by) % count) for i in range(count)])
-
-
-def to_shifted(grid_in):
-    lower_rim = from_behind(grid_in[:SHIFT], "ha", -1)
-    taller = jnp.concatenate([grid_in[SHIFT:], lower_rim], 0)
-    right_rim = from_behind(taller[:, :SHIFT], "wa", -1)
-    return jnp.concatenate([taller[:, SHIFT:], right_rim], 1)
-
-
-def from_shifted(grid_in):
-    upper_rim = from_behind(grid_in[-SHIFT:], "ha", 1)
-    taller = jnp.concatenate([upper_rim, grid_in[:-SHIFT]], 0)
-    left_rim = from_behind(taller[:, -SHIFT:], "wa", 1)
-    return jnp.concatenate([left_rim, taller[:, :-SHIFT]], 1)
-
-
-def to_cells(grid_in, fill):
-    rows, cols, channels = grid_in.shape
-    split = grid_in.reshape(rows // SIDE, SIDE, cols // SIDE, SIDE, channels)
-    extra = CELL - SIDE
-    padded = jnp.pad(
-        split, ((0, 0), (0, extra), (0, 0), (0, extra), (0, 0)), constant_values=fill
-    )
-    return padded.transpose(0, 2, 1, 3, 4).reshape(-1, channels)
-
-
-def from_cells(flat, rows, cols):
-    split = flat.reshape(rows // SIDE, cols // SIDE, CELL, CELL, -1)[:, :, :SIDE, :SIDE]
-    return split.transpose(0, 2, 1, 3, 4).reshape(rows, cols, -1)
 
 
 def normalize(values):
@@ -113,12 +80,6 @@
     for column in range(lanes // LANE):
         block = low[:, column * LANE : (column + 1) * LANE].reshape(high, SUB, LANE)
         tiles_ref[at + column * high : at + (column + 1) * high] = block
-
-
-def from_tiles(tiles_ref, at, rows, column):
-    high = rows // SUB
-    block = tiles_ref[at + column * high : at + (column + 1) * high]
-    return block.reshape(rows, LANE).astype(f32)
 
 
 def strides_of(size):
@@ -152,10 +113,11 @@
 
 
 class Exchange:
-    def __init__(self, streams, sources, sums, landing, totals, send_sem, recv_sem):
+    def __init__(self, streams, sources, sums, landing, totals, send_sem, recv_sem, limits, square_ref):
         self.streams = streams
         self.sources, self.sums, self.landing, self.totals = sources, sums, landing, totals
         self.send_sem, self.recv_sem = send_sem, recv_sem
+        self.limits, self.square_ref = limits, square_ref
         self.rounds = len(streams[0][3])
         self.done = [0] * len(streams)
         self.places = []
@@ -178,14 +140,6 @@
             for link, place in zip(stream[3], places)
         }
 
-    def greet(self):
-        barrier = pltpu.get_barrier_semaphore()
-        for partner in self.partners.values():
-            pl.semaphore_signal(barrier, inc=1, device_id=partner, device_id_type=MESH)
-
-    def meet(self):
-        pl.semaphore_wait(pltpu.get_barrier_semaphore(), len(self.partners))
-
     def arrival(self, index, step):
         _, base, size, _ = self.streams[index]
         return base + size - (size >> step)
@@ -237,7 +191,27 @@
             self.add(index, slot)
         if slot + 1 < 2 * self.rounds:
             self.copy(index, slot + 1).start()
+        if slot == self.rounds - 1:
+            _, keep, _, half = self.places[index][slot]
+            self.square(index, keep, half)
+        elif slot >= self.rounds:
+            _, _, give, half = self.places[index][2 * self.rounds - 1 - slot]
+            self.square(index, give, half)
         self.done[index] = slot + 1
+
+    def square(self, index, first, length):
+        group = self.streams[index][0]
+        totals = self.totals[group]
+        chunk = chunk_of(length)
+
+        def body(i, total):
+            at = first + i * chunk
+            block = totals[pl.ds(at, chunk)].astype(f32)
+            inside = lax.broadcasted_iota(jnp.int32, block.shape, 0) + at < self.limits[group]
+            return total + jnp.sum(jnp.where(inside, block * block, 0.0), 0)
+
+        total = lax.fori_loop(0, length // chunk, body, jnp.zeros((SUB, LANE), f32))
+        self.square_ref[...] += total
 
     def drain(self, order):
         while any(self.done[index] < 2 * self.rounds for index in order):
@@ -250,13 +224,162 @@
                 self.copy(index, slot).wait_send()
 
 
+class Rims:
+    def __init__(self, by, send_sem, recv_sem, phase):
+        spots = {}
+        for axis in ("ha", "wa"):
+            count = lax.axis_size(axis)
+            spots[axis] = (lax.axis_index(axis) + by + count) % count
+        self.targets = ({"ha": spots["ha"]}, {"wa": spots["wa"]}, spots)
+        self.send_sem, self.recv_sem, self.phase = send_sem, recv_sem, phase
+        self.copies = []
+
+    def send(self, which, source, target):
+        at = (self.phase, len(self.copies))
+        copy = pltpu.make_async_remote_copy(
+            src_ref=source,
+            dst_ref=target,
+            send_sem=self.send_sem.at[at],
+            recv_sem=self.recv_sem.at[at],
+            device_id=self.targets[which],
+            device_id_type=MESH,
+        )
+        copy.start()
+        self.copies.append(copy)
+
+    def receive(self):
+        for copy in self.copies:
+            copy.wait_recv()
+
+    def close(self):
+        for copy in self.copies:
+            copy.wait_send()
+
+
+def greet(partners):
+    barrier = pltpu.get_barrier_semaphore()
+    for partner in partners:
+        pl.semaphore_signal(barrier, inc=1, device_id=partner, device_id_type=MESH)
+
+
+def column_of(grid_ref, first, height, layers):
+    return jnp.concatenate([grid_ref[layer, pl.ds(first, height, stride=PITCH), :] for layer in layers], 1)
+
+
+def put_column(grid_ref, first, layers, values):
+    for i, layer in enumerate(layers):
+        part = values[:, i * LANE : (i + 1) * LANE]
+        grid_ref[layer, pl.ds(first, values.shape[0], stride=PITCH), :] = part
+
+
+def rows_at(grid_ref, first, height, layers):
+    return jnp.concatenate([grid_ref[layer, first : first + height, :] for layer in layers], 1)
+
+
+def put_rows(grid_ref, first, layers, values):
+    for i, layer in enumerate(layers):
+        grid_ref[layer, first : first + values.shape[0], :] = values[:, i * LANE : (i + 1) * LANE]
+
+
+def padded_column(column):
+    filler = jnp.zeros((PITCH - column.shape[0], column.shape[1]), f32)
+    return jnp.concatenate([column, filler], 0).astype(bf16)
+
+
+def send_outward(rims, rows_ref, cols_ref, rows_land, cols_land, corner_land, grid_ref, layers, tile):
+    for k in range(SHIFT):
+        rows_ref[k] = rows_at(grid_ref, (tile + k) * PITCH, PITCH, layers).astype(bf16)
+        cols_ref[k] = padded_column(column_of(grid_ref, tile + k, tile + SHIFT, layers))
+    rims.send(0, rows_ref, rows_land)
+    rims.send(1, cols_ref, cols_land)
+    rims.send(2, rows_ref.at[:, pl.ds(PITCH - SUB, SUB)], corner_land)
+
+
+def receive_outward(rims, rows_land, cols_land, corner_land, grid_ref, layers, tile, target_ref):
+    rims.receive()
+    corner = tile - (PITCH - SUB)
+    for k in range(SHIFT):
+        put_rows(grid_ref, k * PITCH, layers, rows_land[k].astype(f32))
+    for k in range(SHIFT):
+        put_column(grid_ref, k, layers, cols_land[k].astype(f32)[: tile + SHIFT])
+    for k in range(SHIFT):
+        put_rows(grid_ref, k * PITCH, layers, corner_land[k].astype(f32)[corner : corner + SHIFT])
+    for row in range(tile):
+        target_ref[row] = rows_at(grid_ref, row * PITCH, tile, layers).astype(bf16)
+
+
+def window_order(rows, cols):
+    spots = [(row, col) for row in range(rows) for col in range(cols)]
+    inner = [spot for spot in spots if spot[0] < rows - 1 and spot[1] < cols - 1]
+    return inner + [spot for spot in spots if spot not in inner], len(inner)
+
+
+def place_of(spot, row):
+    return (spot[0] * SIDE + row + SHIFT) * PITCH + spot[1] * SIDE + SHIFT
+
+
+def cut_windows(grid_ref, cell_ref, order, first, last):
+    inside = lax.broadcasted_iota(jnp.int32, (CELL, LANE), 0) < SIDE
+    for window in range(first, last):
+        for layer in range(grid_ref.shape[0]):
+            rows = []
+            for row in range(SIDE):
+                at = place_of(order[window], row)
+                rows.append(jnp.where(inside, grid_ref[layer, at : at + CELL, :], 0.0))
+            rows.append(jnp.zeros_like(rows[0]))
+            lanes = slice(layer * LANE, (layer + 1) * LANE)
+            cell_ref[window * SLOTS : (window + 1) * SLOTS, lanes] = jnp.concatenate(rows, 0).astype(bf16)
+
+
+def join_windows(values, grid_ref, layers, order):
+    for window, spot in enumerate(order):
+        for row in range(SIDE):
+            place = window * SLOTS + row * CELL
+            put_rows(grid_ref, place_of(spot, row), layers, values[place : place + SIDE])
+
+
+def fill_labels(region_ref, wide_ref, label_ref, order):
+    rows, cols = region_ref.shape
+    wide_ref[:rows, :cols] = region_ref[...].astype(f32)
+    area = wide_ref[: -(-rows // CELL) * CELL, :]
+    lane = lax.broadcasted_iota(jnp.int32, (1, LANE), 1)
+    labels = [jnp.full((1, LANE), -1.0, f32) for _ in order]
+    for col in range(cols // SIDE):
+        for row in range(SIDE):
+            turned = pltpu.roll(area, (row * CELL - col * SIDE) % LANE, 1)
+            inside = (lane >= row * CELL) & (lane < row * CELL + SIDE)
+            for window, spot in enumerate(order):
+                if spot[1] == col:
+                    at = spot[0] * SIDE + row
+                    labels[window] = jnp.where(inside, turned[at : at + 1, :], labels[window])
+    for window in range(len(order)):
+        label_ref[window] = labels[window][:, :SLOTS]
+
+
+def fill_offsets(rel_ref, wide_ref, offset_ref):
+    size = rel_ref.shape[0]
+    wide_ref[:size, :size] = rel_ref[...].astype(f32)
+    lane = lax.broadcasted_iota(jnp.int32, (CELL, LANE), 1)
+    row = lax.broadcasted_iota(jnp.int32, (CELL, LANE), 0)
+    result = jnp.full((CELL, LANE), -1.0, f32)
+    for offset in range(1 - SIDE, SIDE):
+        if offset < 0:
+            turned = pltpu.roll(wide_ref[-offset * SIDE : CELL - offset * SIDE, :], (SIDE + offset) * CELL, 1)
+        else:
+            turned = pltpu.roll(wide_ref[:CELL, :], (SIDE + offset) * CELL - offset * SIDE, 1)
+        first = (SIDE + offset) * CELL
+        result = jnp.where((lane >= first) & (lane < first + SIDE), turned, result)
+    offset_ref[...] = jnp.where(row < SIDE, result, -1.0).astype(jnp.int32)
+
+
 def picks(offset_ref, place):
     labels = lax.broadcasted_iota(jnp.int32, (2 * LANE, LANE), 0)
     return (labels == offset_ref[place : place + 1, :]).astype(f32).astype(bf16)
 
 
-def fill_bias(offset_ref, label_ref, spread_ref, bias_ref):
-    rest = label_ref[...]
+def fill_bias(offset_ref, table_ref, wide_ref, spread_ref, bias_ref):
+    wide_ref[: table_ref.shape[0], : table_ref.shape[1]] = table_ref[...]
+    rest = wide_ref[...]
     parts = []
     for _ in range(3):
         part = rest.astype(bf16)
@@ -292,32 +415,67 @@
 
 
 def block_kernel(
-    windows, streams, slots,
-    cell_ref, region_ref, offset_ref, label_ref, wq_ref, wp_ref, w1_ref, w2_ref,
-    out_ref, grad_ref, early_out, late_out,
+    windows, streams, slots, limits, order, inner,
+    tok_ref, ct_ref, region_in, rel_ref, table_in, wq_ref, wp_ref, w1_ref, w2_ref,
+    out_ref, grad_ref, early_out, late_out, table_out, factor_ref,
+    region_ref, offset_ref, wide_region, wide_rel, wide_table, cell_ref, grid_ref, out_cells, square_ref, in_cols, in_land, in_cols_land, in_corner_land,
+    rows_pack, cols_pack, rows_land, cols_land, corner_land, rim_send, rim_recv,
     bias_ref, spread_ref, scores_ref, normal_ref, qkv_ref, attn_ref, probs_ref, mid_ref, up_ref, gq_ref,
     acc1, acc2, early_in, late_in, early_sum, late_sum, early_land, late_land, send_sem, recv_sem,
 ):
     exchange = Exchange(
         streams, (early_in, late_in), (early_sum, late_sum), (early_land, late_land), (early_out, late_out),
-        send_sem, recv_sem,
+        send_sem, recv_sem, limits, square_ref,
     )
+    rims = [Rims(by, rim_send, rim_recv, phase) for phase, by in enumerate((-1, 1, 1))]
+    partners = list(exchange.partners.values()) + list(rims[0].targets) + list(rims[1].targets)
+    greet(partners)
     early = [index for index, stream in enumerate(streams) if stream[0] == 0]
     late = [index for index, stream in enumerate(streams) if stream[0] == 1]
-    exchange.greet()
-    total_rows, channels = out_ref.shape
-    count = total_rows // SLOTS
+    tile, _, channels = tok_ref.shape
+    count = cell_ref.shape[0] // SLOTS
     block = windows * SLOTS
     hidden_units = w1_ref.shape[1]
     width = hidden_units // FFN_CHUNKS
     stacked_rows = GROUP * SLOTS
     mask = head_mask()
     mask_low = mask.astype(bf16)
-    fill_bias(offset_ref, label_ref, spread_ref, bias_ref)
+    mine = range(channels // LANE)
+    other = range(channels // LANE, 2 * channels // LANE)
+    both = range(2 * channels // LANE)
+    for row in range(tile):
+        put_rows(grid_ref, row * PITCH, mine, tok_ref[row].astype(f32))
+        put_rows(grid_ref, row * PITCH, other, ct_ref[row].astype(f32))
+    for k in range(SHIFT):
+        in_cols[k] = padded_column(column_of(grid_ref, k, tile, both))
+    for wide_ref in (wide_region, wide_rel, wide_table):
+        wide_ref[...] = jnp.zeros_like(wide_ref)
+    fill_labels(region_in, wide_region, region_ref, order)
+    fill_offsets(rel_ref, wide_rel, offset_ref)
+    fill_bias(offset_ref, table_in, wide_table, spread_ref, bias_ref)
+    square_ref[...] = jnp.zeros_like(square_ref)
+    pl.semaphore_wait(pltpu.get_barrier_semaphore(), len(partners))
+    rims[0].send(0, tok_ref.at[pl.ds(0, SHIFT)], in_land.at[0])
+    rims[0].send(0, ct_ref.at[pl.ds(0, SHIFT)], in_land.at[1])
+    rims[0].send(1, in_cols, in_cols_land)
+    rims[0].send(2, in_cols.at[:, pl.ds(0, SUB)], in_corner_land)
+    ready = inner // windows
+    cut_windows(grid_ref, cell_ref, order, 0, ready * windows)
+
+    def take_rims():
+        rims[0].receive()
+        for k in range(SHIFT):
+            put_rows(grid_ref, (tile + k) * PITCH, mine, in_land[0, k].astype(f32))
+            put_rows(grid_ref, (tile + k) * PITCH, other, in_land[1, k].astype(f32))
+            put_column(grid_ref, tile + k, both, in_cols_land[k].astype(f32)[:tile])
+            put_column(grid_ref, tile * PITCH + tile + k, both, in_corner_land[k].astype(f32)[:SHIFT])
+        cut_windows(grid_ref, cell_ref, order, ready * windows, count)
+
     acc1[...] = jnp.zeros_like(acc1)
     acc2[...] = jnp.zeros_like(acc2)
 
     def forward(step, carry):
+        pl.when(step == ready)(take_rims)
         rows = pl.ds(pl.multiple_of(step * block, block), block)
         token = cell_ref[rows, :channels].astype(f32)
         upstream = cell_ref[rows, channels:]
@@ -364,7 +522,7 @@
             grad_pre = (product(upstream, w2, 1, 1) * (cdf + pre * density)).astype(bf16)
             acc1[:, at] += product(low_turned, grad_pre, 1, 0)
             back = back + product(grad_pre, w1, 1, 1)
-        out_ref[rows, :] = total.astype(bf16)
+        out_cells[rows, :] = total
         mid_ref[rows, :] = upstream.astype(f32) + normalize_back(second, scale, back)
         return carry
 
@@ -378,9 +536,11 @@
     used += channels * channels // TILE
     if used < early_in.shape[0]:
         early_in[used:] = jnp.zeros((early_in.shape[0] - used, SUB, LANE), bf16)
-    exchange.meet()
     for index in early:
         exchange.start(index)
+    join_windows(out_cells, grid_ref, mine, order)
+    landings = [(rows_land.at[i], cols_land.at[i], corner_land.at[i]) for i in range(2)]
+    send_outward(rims[1], rows_pack.at[0], cols_pack.at[0], *landings[0], grid_ref, mine, tile)
     up_ref[...] = product(mid_low, wp_ref[...], 1, 1).astype(bf16)
     scores_ref[...] = jnp.zeros_like(scores_ref)
 
@@ -432,51 +592,87 @@
         rows = pl.ds(pl.multiple_of(step * block, block), block)
         normal, scale = normalize(cell_ref[rows, :channels].astype(f32))
         grad_normed = product(gq_ref[rows, :], wq_ref[...], 1, 1).astype(bf16).astype(f32)
-        grad_ref[rows, :] = (mid_ref[rows, :] + normalize_back(normal, scale, grad_normed)).astype(bf16)
+        out_cells[rows, :] = mid_ref[rows, :] + normalize_back(normal, scale, grad_normed)
         return carry
 
     lax.fori_loop(0, count // windows, finish_tokens, 0)
+    join_windows(out_cells, grid_ref, other, order)
+    send_outward(rims[2], rows_pack.at[1], cols_pack.at[1], *landings[1], grid_ref, other, tile)
+    receive_outward(rims[1], *landings[0], grid_ref, mine, tile, out_ref)
+    for index in late + early:
+        exchange.advance(index)
+    receive_outward(rims[2], *landings[1], grid_ref, other, tile, grad_ref)
     exchange.drain(late + early)
-    exchange.close()
-
-
-def finish_kernel(early_ref, late_ref, offset_ref, gq_ref, gp_ref, g1_ref, g2_ref, table_ref):
-    def squares(ref, first, last):
-        chunk = chunk_of(last - first)
-
-        def body(i, total):
-            block = ref[pl.ds(first + i * chunk, chunk)].astype(f32)
-            return total + jnp.sum(block * block, 0)
-
-        return lax.fori_loop(0, (last - first) // chunk, body, jnp.zeros((SUB, LANE), f32))
-
-    used = gq_ref.size // TILE
     table = jnp.zeros((SUB, 2 * LANE), f32)
     for place in range(CELL):
-        table = table + product(late_ref[used + place], picks(offset_ref, place), 1, 1)
-    norm_sq = jnp.sum(squares(early_ref, 0, early_ref.shape[0]) + squares(late_ref, 0, used))
-    norm_sq = norm_sq + jnp.sum(table * table)
+        table = table + product(late_out[limits[1] + place], picks(offset_ref, place), 1, 1)
+    table_out[...] = table
+    norm_sq = jnp.sum(square_ref[...]) + jnp.sum(table * table)
     norm_sq = jnp.full((SUB // 2, LANE), norm_sq, f32)
-    factor = jnp.minimum(1.0, math.sqrt(PARAMS) / (jnp.sqrt(norm_sq) + 1e-06))[:1]
+    factor_ref[...] = jnp.minimum(1.0, math.sqrt(PARAMS) / (jnp.sqrt(norm_sq) + 1e-06))
+    exchange.close()
+    for rim in rims:
+        rim.close()
+
+
+def finish_kernel(
+    pieces, block_in, grad_in, early_ref, late_ref, table_ref, factor_ref,
+    block_out, token_out, gq_ref, gp_ref, g1_ref, g2_ref, table_out,
+    block_full, token_full, tiles, gq_full, gp_full, g1_full, g2_full, in_sem, out_sem,
+):
+    sources = (early_ref, late_ref)
+    results = ((gq_ref, gq_full), (gp_ref, gp_full), (g1_ref, g1_full), (g2_ref, g2_full))
+    loads = []
     at = 0
-    for ref, source in ((g1_ref, early_ref), (g2_ref, early_ref), (gp_ref, early_ref), (gq_ref, late_ref)):
-        at = 0 if ref is gq_ref else at
-        rows, lanes = ref.shape
-        for column in range(lanes // LANE):
-            ref[:, column * LANE : (column + 1) * LANE] = from_tiles(source, at, rows, column) * factor
-        at += ref.size // TILE
-    for column in range(2):
-        lanes = slice(column * LANE, (column + 1) * LANE)
-        table_ref[:, lanes] = table[:, lanes] * factor
-
-
-def offsets_of(rel_index):
-    rel = rel_index.reshape(SIDE, SIDE, SIDE, SIDE)
-    behind = rel[1:, :, 0][::-1]
-    ahead = rel[0].transpose(1, 0, 2)
-    places = jnp.concatenate([behind, ahead], 0).transpose(1, 0, 2)
-    places = jnp.pad(places, ((0, 1), (1, 2), (0, 1)), constant_values=-1)
-    return places.reshape(CELL, LANE)
+    for i, (group, first, length, _, _, _) in enumerate(pieces):
+        load = pltpu.make_async_copy(
+            sources[group].at[pl.ds(first, length)], tiles.at[pl.ds(at, length)], in_sem.at[i]
+        )
+        load.start()
+        loads.append((load, at))
+        at += length
+    passed = ((block_in, block_full, block_out), (grad_in, token_full, token_out))
+    for i, (source, full, _) in enumerate(passed):
+        load = pltpu.make_async_copy(source, full, in_sem.at[len(pieces) + i])
+        load.start()
+        loads.append((load, 0))
+    factor = factor_ref[:1]
+    stores = []
+    for i, (group, first, length, which, column, columns) in enumerate(pieces):
+        load, at = loads[i]
+        load.wait()
+        target, full = results[which]
+        rows = full.shape[0]
+        high = rows // SUB
+        for k in range(columns):
+            block = tiles[at + k * high : at + (k + 1) * high].reshape(rows, LANE).astype(f32)
+            full[:, (column + k) * LANE : (column + k + 1) * LANE] = block * factor
+        lanes = pl.ds(column * LANE, columns * LANE)
+        store = pltpu.make_async_copy(full.at[:, lanes], target.at[:, lanes], out_sem.at[i])
+        store.start()
+        stores.append(store)
+    for i, (_, full, target) in enumerate(passed):
+        loads[len(pieces) + i][0].wait()
+        store = pltpu.make_async_copy(full, target, out_sem.at[len(pieces) + i])
+        store.start()
+        stores.append(store)
+    table = table_ref[...] * jnp.concatenate([factor] * 2, 1)
+    table_out[...] = table[: table_out.shape[0], : table_out.shape[1]]
+    for store in stores:
+        store.wait()
+
+
+def pieces_of(channels, ffn):
+    pieces = []
+    starts = [0, 0]
+    for group, which, rows, lanes, step in (
+        (0, 2, channels, ffn, 3), (0, 3, ffn, channels, 1), (0, 1, channels, channels, 3), (1, 0, channels, 3 * channels, 3),
+    ):
+        for column in range(0, lanes // LANE, step):
+            length = rows // SUB * step
+            pieces.append((group, starts[group], length, which, column, step))
+            starts[group] += length
+    return pieces
 
 
 def local(tokens, cotangent, w_qkv, w_proj, w_fc1, w_fc2, bias_table, rel_index, region):
@@ -486,12 +682,7 @@
     windows = math.gcd(count, 4)
     total = count * SLOTS
 
-    both = to_shifted(jnp.concatenate([tokens, cotangent], -1))
-    cells = to_cells(both, 0)
-    labels = to_cells(region[..., None], -1).astype(f32).reshape(count, 1, SLOTS)
-    offsets = offsets_of(rel_index)
-    label_rows = jnp.pad(bias_table.T, ((0, SUB - HEADS), (0, 2 * LANE - TABLE)))
-
+    order, inner = window_order(tile_rows // SIDE, tile_cols // SIDE)
     across = (lax.axis_size("ha"), lax.axis_size("wa"))
     devices = across[0] * across[1]
     early_tiles = padded_tiles((2 * channels * ffn + channels * channels) // TILE, devices)
@@ -507,54 +698,78 @@
     late = (late_tiles, SUB, LANE)
     in_vmem = pl.BlockSpec(memory_space=pltpu.VMEM)
     semaphores = pltpu.SemaphoreType.DMA((len(streams), 2 * len(orders[0])))
-    vmem_limit = 62 * 1024 * 1024
-    block_cells, grad_cells, early_sum, late_sum = pl.pallas_call(
-        functools.partial(block_kernel, windows, streams, slots),
+    vmem_limit = 63 * 1024 * 1024
+    limits = (early_tiles, 3 * channels * channels // TILE)
+    vmem = pltpu.VMEM
+    summed = pl.pallas_call(
+        functools.partial(block_kernel, windows, streams, slots, limits, order, inner),
         name="block",
         out_shape=[
-            shape((total, channels), bf16), shape((total, channels), bf16), shape(early, bf16), shape(late, bf16),
+            shape(tokens.shape, bf16), shape(tokens.shape, bf16), shape(early, bf16), shape(late, bf16),
+            shape((SUB, 2 * LANE), f32), shape((SUB // 2, LANE), f32),
         ],
-        in_specs=[in_vmem] * 8,
-        out_specs=[in_vmem] * 4,
+        in_specs=[in_vmem] * 9,
+        out_specs=[in_vmem] * 6,
         scratch_shapes=[
-            pltpu.VMEM((HEADS * SLOTS, SLOTS), f32),
-            pltpu.VMEM((HEADS * CELL, LANE), f32),
-            pltpu.VMEM((HEADS * SLOTS, LANE), f32),
-            pltpu.VMEM((total, channels), bf16),
-            pltpu.VMEM((total, 3 * channels), bf16),
-            pltpu.VMEM((total, channels), bf16),
-            pltpu.VMEM((count * HEADS * SLOTS, SLOTS), bf16),
-            pltpu.VMEM((total, channels), f32),
-            pltpu.VMEM((total, channels), bf16),
-            pltpu.VMEM((total, 3 * channels), bf16),
-            pltpu.VMEM((channels, ffn), f32),
-            pltpu.VMEM((channels, ffn), f32),
-        ] + [pltpu.VMEM(group, bf16) for group in (early, late)] * 3 + [semaphores] * 2,
+            vmem((count, 1, SLOTS), f32),
+            vmem((CELL, LANE), jnp.int32),
+            vmem((LANE, LANE), f32),
+            vmem((LANE, LANE), f32),
+            vmem((SUB, 2 * LANE), f32),
+            vmem((total, 2 * channels), bf16),
+            vmem((2 * channels // LANE, (tile_rows + SHIFT) * PITCH, LANE), f32),
+            vmem((total, channels), f32),
+            vmem((SUB, LANE), f32),
+            vmem((SHIFT, PITCH, 2 * channels), bf16),
+            vmem((2, SHIFT, tile_cols, channels), bf16),
+            vmem((SHIFT, PITCH, 2 * channels), bf16),
+            vmem((SHIFT, SUB, 2 * channels), bf16),
+            vmem((2, SHIFT, PITCH, channels), bf16),
+            vmem((2, SHIFT, PITCH, channels), bf16),
+            vmem((2, SHIFT, PITCH, channels), bf16),
+            vmem((2, SHIFT, PITCH, channels), bf16),
+            vmem((2, SHIFT, SUB, channels), bf16),
+            pltpu.SemaphoreType.DMA((3, 4)),
+            pltpu.SemaphoreType.DMA((3, 4)),
+            vmem((HEADS * SLOTS, SLOTS), f32),
+            vmem((HEADS * CELL, LANE), f32),
+            vmem((HEADS * SLOTS, LANE), f32),
+            vmem((total, channels), bf16),
+            vmem((total, 3 * channels), bf16),
+            vmem((total, channels), bf16),
+            vmem((count * HEADS * SLOTS, SLOTS), bf16),
+            vmem((total, channels), f32),
+            vmem((total, channels), bf16),
+            vmem((total, 3 * channels), bf16),
+            vmem((channels, ffn), f32),
+            vmem((channels, ffn), f32),
+        ] + [vmem(group, bf16) for group in (early, late)] * 3 + [semaphores] * 2,
         compiler_params=pltpu.CompilerParams(
             collective_id=0, has_side_effects=True, vmem_limit_bytes=vmem_limit
         ),
         cost_estimate=pl.CostEstimate(
             flops=36_000_000_000, bytes_accessed=20_000_000, transcendentals=5_000_000
         ),
-    )(cells, labels, offsets, label_rows, w_qkv, w_proj, w_fc1, w_fc2)
-    block_out = from_shifted(from_cells(block_cells, tile_rows, tile_cols))
-    token_grad = from_shifted(from_cells(grad_cells, tile_rows, tile_cols))
-
-    gq, gp, g1, g2, table = pl.pallas_call(
-        finish_kernel,
+    )(tokens, cotangent, region, rel_index, bias_table.T, w_qkv, w_proj, w_fc1, w_fc2)
+
+    pieces = pieces_of(channels, ffn)
+    in_place = pl.BlockSpec(memory_space=pl.ANY)
+    results = [(channels, 3 * channels), (channels, channels), (channels, ffn), (ffn, channels)]
+    block_out, token_grad, gq, gp, g1, g2, table = pl.pallas_call(
+        functools.partial(finish_kernel, pieces),
         name="finish",
-        out_shape=[
-            shape((channels, 3 * channels), f32),
-            shape((channels, channels), f32),
-            shape((channels, ffn), f32),
-            shape((ffn, channels), f32),
-            shape((SUB, 2 * LANE), f32),
-        ],
-        in_specs=[in_vmem] * 3,
-        out_specs=[in_vmem] * 5,
+        out_shape=[shape(tokens.shape, bf16)] * 2
+        + [shape(result, f32) for result in results]
+        + [shape(bias_table.T.shape, f32)],
+        in_specs=[in_place] * 4 + [in_vmem] * 2,
+        out_specs=[in_place] * 6 + [in_vmem],
+        scratch_shapes=[vmem(tokens.shape, bf16)] * 2
+        + [vmem((sum(piece[2] for piece in pieces), SUB, LANE), bf16)]
+        + [vmem(result, f32) for result in results]
+        + [pltpu.SemaphoreType.DMA((len(pieces) + 2,))] * 2,
         compiler_params=pltpu.CompilerParams(vmem_limit_bytes=vmem_limit),
-    )(early_sum, late_sum, offsets)
-    return (block_out, token_grad, gq, gp, g1, g2, table[:HEADS, :TABLE].T)
+    )(*summed)
+    return (block_out, token_grad, gq, gp, g1, g2, table.T)
 
 
 def solution(mesh):

time: 129 us -> 103 us (0.80)
  starting transfers between devices: 9.6 us -> 0 us
  local copies, waits for them, and re-layouts: 9.51 us -> 0 us
  waiting for transfers between devices: 8.17 us -> 0 us
  Pallas kernels: 97 us -> 102 us
  other arithmetic: 3.05 us -> 0 us
    ppermute x6 -> x0, starting transfers between devices: 9.6 us -> none  [from_behind(): return lax.ppermute(x, axis, [(i, (i + by) % count) for i in range(count)])]
    ppermute x6 -> x0, waiting for transfers between devices: 8.17 us -> none  [from_behind(): return lax.ppermute(x, axis, [(i, (i + by) % count) for i in range(count)])]
    pallas_call x2, Pallas kernels: 97 us -> 102 us  [the longest x1 95.8 us: local(): pl.pallas_call(functools.partial(block_kernel, windows, streams, slots, l...]
    transpose x5 -> x0, local copies, waits for them, and re-layouts: 4.25 us -> none  [the longest x2 1.6 us: to_cells(): return padded.transpose(0, 2, 1, 3, 4).reshape(-1, channels)]
    concatenate x5 -> x0, other arithmetic: 2.9 us -> none  [the longest x2 2.26 us: from_shifted(): return jnp.concatenate([left_rim, taller[:, :-SHIFT]], 1)]
    reshape x5 -> x0, local copies, waits for them, and re-layouts: 1.6 us -> none  [the longest x1 0.68 us: offsets_of(): return places.reshape(CELL, LANE)]
    unnamed x12 -> x0, local copies, waits for them, and re-layouts: 1.31 us -> none
  transfers between devices with their start and end apart: 6 -> 0, of which waited for: 3 -> 0; matrix products, arithmetic and copies ran while one was open for 4% -> 0% of each run, Pallas kernels for 5% -> 0%
where the time goes in v3:
time: 103 us; the launch traced here: 102 us
  Pallas kernels  102 us (99%)
    pallas_call x1, Pallas kernels, local(): pl.pallas_call(functools.partial(block_kernel, windows, streams, slots, l...  95.8 us
    pallas_call x1, Pallas kernels, local(): pl.pallas_call(functools.partial(finish_kernel, pieces), name='finish', o...  5.91 us

profile of v3, /device:TPU:0, one launch (start us, length us, event | category | flops | bytes accessed | tf_op | source)
XLA Modules:
  0.0 102.4 jit_solution(7619834526632878472)
XLA Ops:
  0.6 95.8 %block.1 = (bf16[28,28,384]{2,1,0:T(8,128)(2,1)}, bf16[28,28,384]{2,1,0:T(8,128)(2,1)}, bf16[672,16,128]{2,1,0:T(8,128)(2,1)}, bf16[224,16,128]{2,1,0:T(8,128)(2...) custom-call(bf16[28,28,384]{2,1,0:T(8,128)(2,1)} %tok_ref.1, bf16[28,28,384]{2,1,0:T(8,128)(2,1)} %ct_ref.1, ...), custom_call_target="tpu_custom_call" | custom-call | flops 35999997952 | bytes 20000000 | tf_op jit(solution)/shard_map/block/pallas_call | solution.py:704
  96.4 5.9 %finish.1 = (bf16[28,28,384]{2,1,0:T(8,128)(2,1)}, bf16[28,28,384]{2,1,0:T(8,128)(2,1)}, f32[384,1152]{1,0:T(8,128)}, f32[384,384]{1,0:T(8,128)}, f32[384,1536]{...) custom-call(bf16[28,28,384]{2,1,0:T(8,128)(2,1)} %get-tuple-element.20.block_in, ...), custom_call_target="tpu_custom_call" | custom-call | tf_op jit(solution)/shard_map/finish/pallas_call | solution.py:758

commit v4 on v3

--- a/solution.py
+++ b/solution.py
@@ -23,9 +23,11 @@
 SUB = 16
 LANE = 128
 TILE = SUB * LANE
-STREAMS = (4, 2)
+EARLY_PLAN = (('a', 4), ('b', 4), ('c', 5), ('a', 4), ('b', 4))
+LATE_PLAN = (('d', 1), ('e', 1))
 PAIR = 2
-SLOT_MOVES = ((), (0, 1, 2, 3), (), (0, 1), (2, 3), (0, 1), (2, 3, 0, 1), (2, 3))
+TOKEN_MOVES = ('e', 'l', '', 'e')
+ROUNDS_BY_SLOT = (0, 1, 1, 1.4, 2, 2.4, 3, 3.4)
 MESH = pl.DeviceIdType.MESH
 PITCH = 32
 
@@ -82,26 +84,57 @@
         tiles_ref[at + column * high : at + (column + 1) * high] = block
 
 
-def strides_of(size):
-    return [1 << i for i in range(size.bit_length() - 1)]
+def digits_of(axis, size, stride, most):
+    digits = []
+    while stride < size:
+        radix = min(most, size // stride)
+        digits.append((axis, stride, radix))
+        stride *= radix
+    return digits
 
 
 def link_orders(across_ha, across_wa):
-    first, *far = [("wa", stride) for stride in strides_of(across_wa)]
-    near = [("ha", stride) for stride in strides_of(across_ha)]
-    return ([first] + near + far, [first] + near[::-1] + far)
-
-
-def split_streams(group, tiles, devices, parts, orders):
+    core = digits_of("wa", 2, 1, 2)
+    near = digits_of("ha", across_ha, 1, 2)
+    near_wide = digits_of("ha", across_ha, 1, 4)
+    far = digits_of("wa", across_wa, 2, 4)
+    far_slim = digits_of("wa", across_wa, 2, 2)
+    orders = {
+        "a": core + near + far,
+        "b": core + near[::-1] + far,
+        "c": core + far + near,
+        "d": core + near_wide + far,
+        "e": core + far + near_wide,
+        "s": core + near + far_slim,
+        "t": core + near[::-1] + far_slim,
+        "u": core + far_slim + near,
+    }
+    return orders
+
+
+def split_streams(group, tiles, devices, plan, orders):
     units = tiles // devices
+    total = sum(weight for _, weight in plan)
     streams = []
     base = 0
-    for part in range(parts):
-        size = (units // parts + (part < units % parts)) * devices
+    passed = 0
+    for name, weight in plan:
+        passed += weight
+        size = (units * passed + total // 2) // total * devices - base
         if size:
-            streams.append((group, base, size, orders[part % len(orders)]))
+            streams.append((group, base, size, orders[name]))
         base += size
     return streams
+
+
+def slot_moves(streams, slots):
+    moves = []
+    done = 0
+    for slot in range(slots):
+        until = int(ROUNDS_BY_SLOT[min(slot, len(ROUNDS_BY_SLOT) - 1)] * streams)
+        moves.append([index % streams for index in range(done, until)])
+        done = max(done, until)
+    return moves
 
 
 def padded_tiles(tiles, devices):
@@ -118,85 +151,95 @@
         self.sources, self.sums, self.landing, self.totals = sources, sums, landing, totals
         self.send_sem, self.recv_sem = send_sem, recv_sem
         self.limits, self.square_ref = limits, square_ref
-        self.rounds = len(streams[0][3])
         self.done = [0] * len(streams)
         self.places = []
+        self.partners = {}
         for group, base, size, order in streams:
             places = []
             low = base
-            for step, (axis, stride) in enumerate(order):
-                half = size >> (step + 1)
+            arrive = base
+            for axis, stride, radix in order:
+                size = size // radix
                 me = lax.axis_index(axis)
-                bit = (me // stride) % 2
-                partner = {axis: me + stride - 2 * stride * bit}
-                keep = low + bit * half
-                give = low + half - bit * half
-                places.append((partner, keep, give, half))
-                low = keep
+                digit = (me // stride) % radix
+                sends = []
+                for k in range(1, radix):
+                    ahead = (digit + k) % radix
+                    behind = (digit + radix - k) % radix
+                    partner = {axis: me + (ahead - digit) * stride}
+                    self.partners[axis, stride, radix, k] = partner
+                    sends.append((partner, low + ahead * size, low + behind * size, arrive))
+                    arrive += size
+                low = low + digit * size
+                places.append((low, size, sends))
             self.places.append(places)
-        self.partners = {
-            link: place[0]
-            for stream, places in zip(streams, self.places)
-            for link, place in zip(stream[3], places)
-        }
-
-    def arrival(self, index, step):
-        _, base, size, _ = self.streams[index]
-        return base + size - (size >> step)
-
-    def copy(self, index, slot):
+
+    def rounds(self, index):
+        return len(self.places[index])
+
+    def copies(self, index, slot):
         group = self.streams[index][0]
-        if slot < self.rounds:
-            partner, _, give, half = self.places[index][slot]
-            source = (self.sums if slot else self.sources)[group].at[pl.ds(give, half)]
-            target = self.landing[group].at[pl.ds(self.arrival(index, slot), half)]
-        else:
-            partner, keep, _, half = self.places[index][2 * self.rounds - 1 - slot]
-            source = self.totals[group].at[pl.ds(keep, half)]
-            target = source
-        return pltpu.make_async_remote_copy(
-            src_ref=source,
-            dst_ref=target,
-            send_sem=self.send_sem.at[index, slot],
-            recv_sem=self.recv_sem.at[index, slot],
-            device_id=partner,
-            device_id_type=MESH,
-        )
+        rounds = self.rounds(index)
+        keep, size, sends = self.places[index][slot if slot < rounds else 2 * rounds - 1 - slot]
+        result = []
+        for k, (partner, give, _, arrive) in enumerate(sends):
+            if slot < rounds:
+                source = (self.sums if slot else self.sources)[group].at[pl.ds(give, size)]
+                target = self.landing[group].at[pl.ds(arrive, size)]
+            else:
+                source = self.totals[group].at[pl.ds(keep, size)]
+                target = source
+            result.append(
+                pltpu.make_async_remote_copy(
+                    src_ref=source,
+                    dst_ref=target,
+                    send_sem=self.send_sem.at[index, slot, k],
+                    recv_sem=self.recv_sem.at[index, slot, k],
+                    device_id=partner,
+                    device_id_type=MESH,
+                )
+            )
+        return result
 
     def add(self, index, step):
         group = self.streams[index][0]
-        _, keep, _, half = self.places[index][step]
+        keep, size, sends = self.places[index][step]
         source = (self.sums if step else self.sources)[group]
-        target = (self.sums if step < self.rounds - 1 else self.totals)[group]
+        target = (self.sums if step < self.rounds(index) - 1 else self.totals)[group]
         landing = self.landing[group]
-        arrive = self.arrival(index, step)
-        chunk = chunk_of(half)
+        chunk = chunk_of(size)
 
         def body(i, carry):
             at = pl.ds(keep + i * chunk, chunk)
-            target[at] = source[at] + landing[pl.ds(arrive + i * chunk, chunk)]
+            total = source[at].astype(f32)
+            for _, _, _, arrive in sends:
+                total = total + landing[pl.ds(arrive + i * chunk, chunk)].astype(f32)
+            target[at] = total.astype(bf16)
             return carry
 
-        lax.fori_loop(0, half // chunk, body, 0)
-
-    def start(self, index):
-        self.copy(index, 0).start()
+        lax.fori_loop(0, size // chunk, body, 0)
+
+    def start(self, index, slot=0):
+        for copy in self.copies(index, slot):
+            copy.start()
 
     def advance(self, index):
         slot = self.done[index]
-        if slot == 2 * self.rounds:
+        rounds = self.rounds(index)
+        if slot == 2 * rounds:
             return
-        self.copy(index, slot).wait_recv()
-        if slot < self.rounds:
+        for copy in self.copies(index, slot):
+            copy.wait_recv()
+        if slot < rounds:
             self.add(index, slot)
-        if slot + 1 < 2 * self.rounds:
-            self.copy(index, slot + 1).start()
-        if slot == self.rounds - 1:
-            _, keep, _, half = self.places[index][slot]
-            self.square(index, keep, half)
-        elif slot >= self.rounds:
-            _, _, give, half = self.places[index][2 * self.rounds - 1 - slot]
-            self.square(index, give, half)
+        if slot + 1 < 2 * rounds:
+            self.start(index, slot + 1)
+        keep, size, sends = self.places[index][slot if slot < rounds else 2 * rounds - 1 - slot]
+        if slot == rounds - 1:
+            self.square(index, keep, size)
+        elif slot >= rounds:
+            for _, _, behind, _ in sends:
+                self.square(index, behind, size)
         self.done[index] = slot + 1
 
     def square(self, index, first, length):
@@ -214,14 +257,15 @@
         self.square_ref[...] += total
 
     def drain(self, order):
-        while any(self.done[index] < 2 * self.rounds for index in order):
+        while any(self.done[index] < 2 * self.rounds(index) for index in order):
             for index in order:
                 self.advance(index)
 
     def close(self):
         for index in range(len(self.streams)):
-            for slot in range(2 * self.rounds):
-                self.copy(index, slot).wait_send()
+            for slot in range(2 * self.rounds(index)):
+                for copy in self.copies(index, slot):
+                    copy.wait_send()
 
 
 class Rims:
@@ -589,6 +633,12 @@
         exchange.start(index)
 
     def finish_tokens(step, carry):
+        for slot, moves in enumerate(TOKEN_MOVES):
+            @pl.when(step == slot)
+            def _(moves=moves):
+                for index in [index for name in moves for index in (late if name == "l" else early)]:
+                    exchange.advance(index)
+
         rows = pl.ds(pl.multiple_of(step * block, block), block)
         normal, scale = normalize(cell_ref[rows, :channels].astype(f32))
         grad_normed = product(gq_ref[rows, :], wq_ref[...], 1, 1).astype(bf16).astype(f32)
@@ -598,6 +648,8 @@
     lax.fori_loop(0, count // windows, finish_tokens, 0)
     join_windows(out_cells, grid_ref, other, order)
     send_outward(rims[2], rows_pack.at[1], cols_pack.at[1], *landings[1], grid_ref, other, tile)
+    for index in late + early:
+        exchange.advance(index)
     receive_outward(rims[1], *landings[0], grid_ref, mine, tile, out_ref)
     for index in late + early:
         exchange.advance(index)
@@ -677,6 +729,7 @@
 
 def local(tokens, cotangent, w_qkv, w_proj, w_fc1, w_fc2, bias_table, rel_index, region):
     tile_rows, tile_cols, channels = tokens.shape
+    assert tile_rows == tile_cols and tile_cols + SHIFT < PITCH
     ffn = w_fc1.shape[1]
     count = (tile_rows // SIDE) * (tile_cols // SIDE)
     windows = math.gcd(count, 4)
@@ -688,16 +741,17 @@
     early_tiles = padded_tiles((2 * channels * ffn + channels * channels) // TILE, devices)
     late_tiles = padded_tiles(3 * channels * channels // TILE + CELL, devices)
     orders = link_orders(*across)
-    streams = split_streams(0, early_tiles, devices, STREAMS[0], orders)
+    streams = split_streams(0, early_tiles, devices, EARLY_PLAN, orders)
     early_count = len(streams)
-    streams += split_streams(1, late_tiles, devices, STREAMS[1], orders)
-    slots = [[index for index in moves if index < early_count] for moves in SLOT_MOVES[: count // PAIR]]
+    streams += split_streams(1, late_tiles, devices, LATE_PLAN, orders)
+    slots = slot_moves(early_count, count // PAIR)
+    most = max(2 * len(stream[3]) for stream in streams)
 
     shape = jax.ShapeDtypeStruct
     early = (early_tiles, SUB, LANE)
     late = (late_tiles, SUB, LANE)
     in_vmem = pl.BlockSpec(memory_space=pltpu.VMEM)
-    semaphores = pltpu.SemaphoreType.DMA((len(streams), 2 * len(orders[0])))
+    semaphores = pltpu.SemaphoreType.DMA((len(streams), most, 3))
     vmem_limit = 63 * 1024 * 1024
     limits = (early_tiles, 3 * channels * channels // TILE)
     vmem = pltpu.VMEM

time: 103 us -> 93.2 us (0.905)
  Pallas kernels: 102 us -> 91.8 us
    pallas_call x1, Pallas kernels: 95.8 us -> 85.9 us  [local(): pl.pallas_call(functools.partial(block_kernel, windows, streams, slots, l...]
where the time goes in v4:
time: 93.2 us; the launch traced here: 92.4 us
  Pallas kernels  91.8 us (98%)
    pallas_call x1, Pallas kernels, local(): pl.pallas_call(functools.partial(block_kernel, windows, streams, slots, l...  85.9 us
    pallas_call x1, Pallas kernels, local(): pl.pallas_call(functools.partial(finish_kernel, pieces), name='finish', o...  5.91 us

profile of v4, /device:TPU:0, one launch (start us, length us, event | category | flops | bytes accessed | tf_op | source)
XLA Modules:
  0.0 92.4 jit_solution(5569123268277190554)
XLA Ops:
  0.6 85.9 %block.1 = (bf16[28,28,384]{2,1,0:T(8,128)(2,1)}, bf16[28,28,384]{2,1,0:T(8,128)(2,1)}, bf16[672,16,128]{2,1,0:T(8,128)(2,1)}, bf16[224,16,128]{2,1,0:T(8,128)(2...) custom-call(bf16[28,28,384]{2,1,0:T(8,128)(2,1)} %tok_ref.1, bf16[28,28,384]{2,1,0:T(8,128)(2,1)} %ct_ref.1, ...), custom_call_target="tpu_custom_call" | custom-call | flops 35999997952 | bytes 20000000 | tf_op jit(solution)/shard_map/block/pallas_call | solution.py:758
  86.5 5.9 %finish.1 = (bf16[28,28,384]{2,1,0:T(8,128)(2,1)}, bf16[28,28,384]{2,1,0:T(8,128)(2,1)}, f32[384,1152]{1,0:T(8,128)}, f32[384,384]{1,0:T(8,128)}, f32[384,1536]{...) custom-call(bf16[28,28,384]{2,1,0:T(8,128)(2,1)} %get-tuple-element.20.block_in, ...), custom_call_target="tpu_custom_call" | custom-call | tf_op jit(solution)/shard_map/finish/pallas_call | solution.py:812

commit v5 on v4

--- a/solution.py
+++ b/solution.py
@@ -27,7 +27,7 @@
 LATE_PLAN = (('d', 1), ('e', 1))
 PAIR = 2
 TOKEN_MOVES = ('e', 'l', '', 'e')
-ROUNDS_BY_SLOT = (0, 1, 1, 1.4, 2, 2.4, 3, 3.4)
+ROUNDS_BY_SLOT = (0, 1, 1, 1.2, 1.8, 2.4, 3, 3.4)
 MESH = pl.DeviceIdType.MESH
 PITCH = 32
 
@@ -358,6 +358,20 @@
     return inner + [spot for spot in spots if spot not in inner], len(inner)
 
 
+def pack_rows(values):
+    count = values.shape[0] // SLOTS
+    return jnp.concatenate([values[w * SLOTS : w * SLOTS + SIDE * CELL] for w in range(count)], 0)
+
+
+def unpack_rows(values):
+    height = SIDE * CELL
+    filler = jnp.zeros((SLOTS - height, values.shape[1]), values.dtype)
+    parts = []
+    for w in range(values.shape[0] // height):
+        parts += [values[w * height : (w + 1) * height], filler]
+    return jnp.concatenate(parts, 0)
+
+
 def place_of(spot, row):
     return (spot[0] * SIDE + row + SHIFT) * PITCH + spot[1] * SIDE + SHIFT
 
@@ -460,9 +474,9 @@
 
 def block_kernel(
     windows, streams, slots, limits, order, inner,
-    tok_ref, ct_ref, region_in, rel_ref, table_in, wq_ref, wp_ref, w1_ref, w2_ref,
+    tok_ref, ct_ref, region_in, rel_ref, table_in, wq_in, wp_in, w1_in, w2_in,
     out_ref, grad_ref, early_out, late_out, table_out, factor_ref,
-    region_ref, offset_ref, wide_region, wide_rel, wide_table, cell_ref, grid_ref, out_cells, square_ref, in_cols, in_land, in_cols_land, in_corner_land,
+    wq_ref, wp_ref, w1_ref, w2_ref, weight_sem, region_ref, offset_ref, wide_region, wide_rel, wide_table, cell_ref, grid_ref, out_cells, square_ref, in_cols, in_land, in_cols_land, in_corner_land,
     rows_pack, cols_pack, rows_land, cols_land, corner_land, rim_send, rim_recv,
     bias_ref, spread_ref, scores_ref, normal_ref, qkv_ref, attn_ref, probs_ref, mid_ref, up_ref, gq_ref,
     acc1, acc2, early_in, late_in, early_sum, late_sum, early_land, late_land, send_sem, recv_sem,
@@ -476,6 +490,12 @@
     greet(partners)
     early = [index for index, stream in enumerate(streams) if stream[0] == 0]
     late = [index for index, stream in enumerate(streams) if stream[0] == 1]
+    weights = [
+        pltpu.make_async_copy(source, target, weight_sem.at[i])
+        for i, (source, target) in enumerate(((wq_in, wq_ref), (wp_in, wp_ref), (w1_in, w1_ref), (w2_in, w2_ref)))
+    ]
+    for weight in weights:
+        weight.start()
     tile, _, channels = tok_ref.shape
     count = cell_ref.shape[0] // SLOTS
     block = windows * SLOTS
@@ -515,6 +535,8 @@
             put_column(grid_ref, tile * PITCH + tile + k, both, in_corner_land[k].astype(f32)[:SHIFT])
         cut_windows(grid_ref, cell_ref, order, ready * windows, count)
 
+    for weight in weights:
+        weight.wait()
     acc1[...] = jnp.zeros_like(acc1)
     acc2[...] = jnp.zeros_like(acc2)
 
@@ -522,7 +544,7 @@
         pl.when(step == ready)(take_rims)
         rows = pl.ds(pl.multiple_of(step * block, block), block)
         token = cell_ref[rows, :channels].astype(f32)
-        upstream = cell_ref[rows, channels:]
+        upstream = pack_rows(cell_ref[rows, channels:].astype(f32)).astype(bf16)
         normal, _ = normalize(token)
         normal_low = normal.astype(bf16)
         normal_ref[rows, :] = normal_low
@@ -546,7 +568,7 @@
                 mixed = product(probs, value, 1, 0)
                 attn_ref[at, lanes : lanes + LANES] = gather_heads(mixed, mask).astype(bf16)
         projected = product(attn_ref[rows, :], wp_ref[...], 1, 0).astype(bf16)
-        middle = token + projected.astype(f32)
+        middle = pack_rows(token + projected.astype(f32))
         second, scale = normalize(middle)
         low = second.astype(bf16)
         low_turned = low.T
@@ -566,8 +588,8 @@
             grad_pre = (product(upstream, w2, 1, 1) * (cdf + pre * density)).astype(bf16)
             acc1[:, at] += product(low_turned, grad_pre, 1, 0)
             back = back + product(grad_pre, w1, 1, 1)
-        out_cells[rows, :] = total
-        mid_ref[rows, :] = upstream.astype(f32) + normalize_back(second, scale, back)
+        out_cells[rows, :] = unpack_rows(total)
+        mid_ref[rows, :] = unpack_rows(upstream.astype(f32) + normalize_back(second, scale, back))
         return carry
 
     lax.fori_loop(0, count // windows, forward, 0)
@@ -623,14 +645,20 @@
     lax.fori_loop(0, count // PAIR, backward, 0)
 
     normal_turned = normal_ref[...].T
-    to_tiles(product(normal_turned, gq_ref[...], 1, 0), late_in, 0)
+    to_tiles(product(normal_turned, gq_ref[:, : 2 * channels], 1, 0), late_in, 0)
+    used = 2 * channels * channels // TILE
+    first_late = [index for index in late if streams[index][1] + streams[index][2] <= used]
+    for index in first_late:
+        exchange.start(index)
+    to_tiles(product(normal_turned, gq_ref[:, 2 * channels :], 1, 0), late_in, used)
     used = 3 * channels * channels // TILE
     gather_offsets(scores_ref, spread_ref, late_in, used)
     used += CELL
     if used < late_in.shape[0]:
         late_in[used:] = jnp.zeros((late_in.shape[0] - used, SUB, LANE), bf16)
     for index in late:
-        exchange.start(index)
+        if index not in first_late:
+            exchange.start(index)
 
     def finish_tokens(step, carry):
         for slot, moves in enumerate(TOKEN_MOVES):
@@ -762,9 +790,14 @@
             shape(tokens.shape, bf16), shape(tokens.shape, bf16), shape(early, bf16), shape(late, bf16),
             shape((SUB, 2 * LANE), f32), shape((SUB // 2, LANE), f32),
         ],
-        in_specs=[in_vmem] * 9,
+        in_specs=[in_vmem] * 5 + [pl.BlockSpec(memory_space=pl.ANY)] * 4,
         out_specs=[in_vmem] * 6,
         scratch_shapes=[
+            vmem(w_qkv.shape, bf16),
+            vmem(w_proj.shape, bf16),
+            vmem(w_fc1.shape, bf16),
+            vmem(w_fc2.shape, bf16),
+            pltpu.SemaphoreType.DMA((4,)),
             vmem((count, 1, SLOTS), f32),
             vmem((CELL, LANE), jnp.int32),
             vmem((LANE, LANE), f32),

time: 93.2 us -> 91.7 us (0.984)
  Pallas kernels: 91.8 us -> 90.2 us
    pallas_call x1, Pallas kernels: 85.9 us -> 84.3 us  [local(): pl.pallas_call(functools.partial(block_kernel, windows, streams, slots, l...]
where the time goes in v5:
time: 91.7 us; the launch traced here: 90.9 us
  Pallas kernels  90.2 us (98%)
    pallas_call x1, Pallas kernels, local(): pl.pallas_call(functools.partial(block_kernel, windows, streams, slots, l...  84.3 us
    pallas_call x1, Pallas kernels, local(): pl.pallas_call(functools.partial(finish_kernel, pieces), name='finish', o...  5.91 us

profile of v5, /device:TPU:0, one launch (start us, length us, event | category | flops | bytes accessed | tf_op | source)
XLA Modules:
  0.0 90.9 jit_solution(15267065910267446956)
XLA Ops:
  0.6 84.3 %block.1 = (bf16[28,28,384]{2,1,0:T(8,128)(2,1)}, bf16[28,28,384]{2,1,0:T(8,128)(2,1)}, bf16[672,16,128]{2,1,0:T(8,128)(2,1)}, bf16[224,16,128]{2,1,0:T(8,128)(2...) custom-call(bf16[28,28,384]{2,1,0:T(8,128)(2,1)} %tok_ref.1, bf16[28,28,384]{2,1,0:T(8,128)(2,1)} %ct_ref.1, ...), custom_call_target="tpu_custom_call" | custom-call | flops 35999997952 | bytes 20000000 | tf_op jit(solution)/shard_map/block/pallas_call | solution.py:786
  85.0 5.9 %finish.1 = (bf16[28,28,384]{2,1,0:T(8,128)(2,1)}, bf16[28,28,384]{2,1,0:T(8,128)(2,1)}, f32[384,1152]{1,0:T(8,128)}, f32[384,384]{1,0:T(8,128)}, f32[384,1536]{...) custom-call(bf16[28,28,384]{2,1,0:T(8,128)(2,1)} %get-tuple-element.20.block_in, ...), custom_call_target="tpu_custom_call" | custom-call | tf_op jit(solution)/shard_map/finish/pallas_call | solution.py:845
